TPU v7x, 32 devices: a whole 2x2x4 slice. The times are simulated.
32 devices in a mesh: ep: 16 (over z, y, x), tp: 2 (over core).
Axes of the slice: x: 2, y: 2, z: 4, core: 2. Of those that a mesh axis runs over, the one named last changes fastest.
Arguments:
- tokens: bfloat16 [2048, 3584], P('ep', 'tp'), may hold values from -6 to 6
- routes: int32 [2048, 8], P('ep'), may hold values from 0 to 15, all different within a row; in each aligned block of 128 rows (0 to 127, 128 to 255, ...) at most 72 rows name the same one
- gate_levels: int32 [2048, 8], P('ep'), may hold values from 1 to 255
- w_gate: bfloat16 [16, 3584, 1024], P('ep', 'tp'), may hold values from -0.09375 to 0.09375
- w_up: bfloat16 [16, 3584, 1024], P('ep', 'tp'), may hold values from -0.09375 to 0.09375
- w_down: bfloat16 [16, 1024, 3584], P('ep', None, 'tp'), may hold values from -0.1875 to 0.1875
Outputs:
- mixed: bfloat16 [2048, 3584], P('ep', 'tp')
Inputs may be any that keep to these rules, and one draw needn't show every extreme that they name: `routes`: each row names 8 different experts. Among the 128 tokens of one aligned block no expert is named by more than 72 rows, and in every draw some expert is named by exactly 72 rows of some block.
All inputs are finite; a program needn't handle non-finite values.
Results may differ from a plain program's by a relative error of at most 0.0085.
Values may be sent and summed in bfloat16 or wider, within the bound.
No kernel may reach another device: no remote copies, remote signals or barrier semaphores. Data moves between devices by JAX's collectives and lax.ppermute only.
A program may use at most 64 MiB of HBM per device.

v0:
```python
import jax
import jax.numpy as jnp
from jax import lax
from jax.experimental import pallas as pl
from jax.experimental.pallas import tpu as pltpu
from jax.sharding import PartitionSpec as P


F32 = jnp.float32
BF16 = jnp.bfloat16
LANES = 128
MIB = 1 << 20
PIECES = 4


def vmem(count):
    return [pl.BlockSpec(memory_space=pltpu.VMEM)] * count


def hbm(count):
    return [pl.BlockSpec(memory_space=pltpu.HBM)] * count


def from_hbm(value):
    return pltpu.with_memory_space_constraint(value, pltpu.HBM)


def params(limit):
    return pltpu.CompilerParams(vmem_limit_bytes=limit * MIB)


def cost(flops, moved):
    return pl.CostEstimate(flops=flops, bytes_accessed=moved, transcendentals=0)


def inner_size(count):
    size = 1
    while size * size < count and count % (2 * size) == 0:
        size *= 2
    return size


def load(value):
    rows = value.shape[0] // PIECES

    def body(src_ref, dst_ref, sems):
        copies = [
            pltpu.make_async_copy(
                src_ref.at[pl.ds(p * rows, rows)], dst_ref.at[pl.ds(p * rows, rows)], sems.at[p]
            )
            for p in range(PIECES)
        ]
        for copy in copies:
            copy.start()
        for copy in copies:
            copy.wait()

    return pl.pallas_call(
        body,
        out_shape=pltpu.VMEM(value.shape, value.dtype),
        in_specs=hbm(1),
        out_specs=vmem(1)[0],
        scratch_shapes=[pltpu.SemaphoreType.DMA((PIECES,))],
        compiler_params=params(2),
        name="load",
    )(from_hbm(value))


def stage(tokens, routes, gate_levels):
    tok_rows, width = tokens.shape
    top = routes.shape[1]
    direct = width % LANES == 0

    def body(routes_ref, levels_ref, tokens_ref, out_ref, held, small, sems):
        target = out_ref.at[:, :width] if direct else held
        copies = [
            pltpu.make_async_copy(routes_ref, small.at[0], sems.at[0]),
            pltpu.make_async_copy(levels_ref, small.at[1], sems.at[1]),
            pltpu.make_async_copy(tokens_ref, target, sems.at[2]),
        ]
        for copy in copies:
            copy.start()
        lane = lax.broadcasted_iota(jnp.int32, (top, LANES), 1)
        choice = lax.broadcasted_iota(jnp.int32, (top, LANES), 0)
        marks = jnp.zeros((tok_rows, LANES), F32)
        for i in range(2):
            copies[i].wait()
            spread = jnp.where(lane == choice + i * top, 1.0, 0.0).astype(BF16)
            marks = marks + lax.dot_general(
                small[i].astype(F32).astype(BF16),
                spread,
                (((0,), (0,)), ((), ())),
                preferred_element_type=F32,
            )
        out_ref[:, width:] = marks.astype(BF16)
        copies[2].wait()
        if not direct:
            out_ref[:, :width] = held[...]

    return pl.pallas_call(
        body,
        out_shape=jax.ShapeDtypeStruct((tok_rows, width + LANES), BF16),
        in_specs=hbm(3),
        out_specs=vmem(1)[0],
        scratch_shapes=[
            pltpu.VMEM((8, LANES) if direct else (tok_rows, width), BF16),
            pltpu.VMEM((2, top, tok_rows), jnp.int32),
            pltpu.SemaphoreType.DMA((3,)),
        ],
        compiler_params=params(8),
        name="stage",
    )(from_hbm(routes.T), from_hbm(gate_levels.T), from_hbm(tokens))


def pack(blocks, width, top, capacity, inner, outer):
    tok_rows = blocks[0].shape[0]
    span = -(-capacity // LANES) * LANES
    count = len(blocks)

    def body(*refs):
        block_refs, mix_ref, out_refs = refs[:count], refs[count], refs[count + 1 :]
        index = lax.axis_index("ep")
        plane, spot = index // inner, index % inner
        block = block_refs[0][...]
        if count == 2:
            middle = (plane > 0) & (plane < outer - 1)
            block = jnp.where(middle, block, block_refs[1][...])
        marks = block[:, width:].astype(F32)
        lane = lax.broadcasted_iota(jnp.int32, marks.shape, 1)
        levels = pltpu.roll(marks, marks.shape[1] - top, 1)
        inside = lane < top
        total = jnp.sum(jnp.where(inside, levels, 0.0), axis=1, keepdims=True)
        named, share = [], []
        gathered = jnp.zeros(marks.shape, F32)
        for j in range(inner):
            hit = inside & (marks == (plane * inner + (spot ^ j)).astype(F32))
            found = jnp.sum(jnp.where(hit, 1.0, 0.0), axis=1, keepdims=True)
            named.append(found)
            share.append(jnp.sum(jnp.where(hit, levels, 0.0), axis=1, keepdims=True) / total)
            gathered = jnp.where(lane == j, found, gathered)
        row = lax.broadcasted_iota(jnp.int32, (tok_rows, tok_rows), 0)
        col = lax.broadcasted_iota(jnp.int32, (tok_rows, tok_rows), 1)
        below = jnp.where(col < row, 1.0, 0.0).astype(BF16)
        slots = jnp.dot(below, gathered.astype(BF16), preferred_element_type=F32)
        place = lax.broadcasted_iota(jnp.int32, (tok_rows, span), 1).astype(F32)
        data = block[:, :width]
        for j in range(inner):
            match = (place == slots[:, j : j + 1]) & (named[j] > 0.0)
            mix_ref[:, j * span : (j + 1) * span] = jnp.where(match, share[j], 0.0).astype(BF16)
            pick = jnp.where(match, 1.0, 0.0).astype(BF16)
            rows = lax.dot_general(
                pick, data, (((0,), (0,)), ((), ())), preferred_element_type=F32
            )
            out_refs[j][...] = rows[:capacity].astype(BF16)

    out = pl.pallas_call(
        body,
        out_shape=[jax.ShapeDtypeStruct((tok_rows, inner * span), BF16)]
        + [jax.ShapeDtypeStruct((capacity, width), BF16)] * inner,
        in_specs=vmem(count),
        out_specs=vmem(1 + inner),
        compiler_params=params(8),
        cost_estimate=cost(2 * inner * span * tok_rows * width, 2 * 3 * tok_rows * width),
        name="pack",
    )(*blocks)
    return out[0], list(out[1:])


def lift(rows, w_gate, w_up, away):
    capacity, width = rows[0].shape
    count = len(rows)
    half = w_gate.shape[1] // 2
    total = count * capacity
    kind = BF16 if away else F32

    def body(*refs):
        in_refs, (gate_ref, up_ref, out_ref, held) = refs[:count], refs[count:]
        for j in range(count):
            held[j * capacity : (j + 1) * capacity, :] = in_refs[j][...]
        side = lax.axis_index("tp")
        at = pl.multiple_of((1 - side if away else side) * half, LANES)
        data = held[...]
        for i, w_ref in enumerate((gate_ref, up_ref)):
            out_ref[:, i * half : (i + 1) * half] = jnp.dot(
                data, w_ref[:, pl.ds(at, half)], preferred_element_type=F32
            ).astype(kind)

    return pl.pallas_call(
        body,
        out_shape=jax.ShapeDtypeStruct((total, 2 * half), kind),
        in_specs=vmem(count + 2),
        out_specs=vmem(1)[0],
        scratch_shapes=[pltpu.VMEM((total, width), BF16)],
        compiler_params=params(8),
        cost_estimate=cost(4 * total * width * half, 4 * width * half),
        name="lift",
    )(*rows, w_gate, w_up)


def activate(keep, got):
    total, wide = keep.shape
    half = wide // 2

    def body(keep_ref, got_ref, out_ref):
        gate = keep_ref[:, :half] + got_ref[:, :half].astype(F32)
        up = keep_ref[:, half:] + got_ref[:, half:].astype(F32)
        out_ref[...] = (gate / (1.0 + jnp.exp(-gate)) * up).astype(BF16)

    return pl.pallas_call(
        body,
        out_shape=jax.ShapeDtypeStruct((total, half), BF16),
        in_specs=vmem(2),
        out_specs=vmem(1)[0],
        compiler_params=params(8),
        cost_estimate=cost(20 * total * half, 8 * total * half),
        name="activate",
    )(keep, got)


def lower(own, other, w_down, count):
    total, half = own.shape
    width = w_down.shape[1]
    capacity = total // count

    def body(own_ref, other_ref, w_ref, *out_refs):
        side = lax.axis_index("tp")
        mine = pl.multiple_of(side * half, LANES)
        theirs = pl.multiple_of((1 - side) * half, LANES)
        out = jnp.dot(own_ref[...], w_ref[pl.ds(mine, half), :], preferred_element_type=F32)
        out = out + jnp.dot(
            other_ref[...], w_ref[pl.ds(theirs, half), :], preferred_element_type=F32
        )
        for j in range(count):
            out_refs[j][...] = out[j * capacity : (j + 1) * capacity].astype(BF16)

    return pl.pallas_call(
        body,
        out_shape=[jax.ShapeDtypeStruct((capacity, width), BF16)] * count,
        in_specs=vmem(3),
        out_specs=vmem(count),
        compiler_params=params(16),
        cost_estimate=cost(4 * total * half * width, 4 * half * width),
        name="lower",
    )(own, other, w_down)


def combine(rows, mix, partials, out_type):
    capacity, width = rows[0].shape
    count = len(rows)
    tok_rows = mix.shape[0]
    span = mix.shape[1] // count

    def body(mix_ref, *refs):
        total = None
        for j in range(count):
            term = jnp.dot(
                mix_ref[:, j * span : j * span + capacity],
                refs[j][...],
                preferred_element_type=F32,
            )
            total = term if total is None else total + term
        for ref in refs[count:-1]:
            total = total + ref[...].astype(F32)
        refs[-1][...] = total.astype(out_type)

    return pl.pallas_call(
        body,
        out_shape=jax.ShapeDtypeStruct((tok_rows, width), out_type),
        in_specs=vmem(1 + count + len(partials)),
        out_specs=vmem(1)[0],
        compiler_params=params(10),
        cost_estimate=cost(2 * count * capacity * tok_rows * width, 2 * tok_rows * width),
        name="combine",
    )(mix, *rows, *partials)


def on_device(tokens, routes, gate_levels, w_gate, w_up, w_down):
    ep_count, tp_count = lax.axis_size("ep"), lax.axis_size("tp")
    tok_rows, top_count = routes.shape
    assert w_gate.shape[0] == 1
    w_gate, w_up, w_down = w_gate[0], w_up[0], w_down[0]
    capacity = min(tok_rows, max(2, 9 * tok_rows * top_count // (8 * ep_count)))
    width = tokens.shape[1]
    inner = inner_size(ep_count)
    outer = ep_count // inner

    def hop(value, hops):
        pairs = [(a * inner + i, b * inner + i) for a, b in hops for i in range(inner)]
        return lax.ppermute(value, "ep", pairs)

    def flip(value, step):
        pairs = [(i, (i // inner ^ step) * inner + i % inner) for i in range(ep_count)]
        return lax.ppermute(value, "ep", pairs)

    def near(rows):
        out = [rows[0]]
        for j in range(1, inner):
            out.append(lax.ppermute(rows[j], "ep", [(i, i ^ j) for i in range(ep_count)]))
        return out

    def swap(value):
        return lax.ppermute(value, "tp", [(0, 1), (1, 0)])

    def send(blocks):
        mix, packed = pack(blocks, width, top_count, capacity, inner, outer)
        return mix, near(packed)

    def expert(rows, w_gate, w_up, w_down):
        if tp_count == 2:
            give = lift(rows, w_gate, w_up, True)
            got = swap(give)
            keep = lift(rows, w_gate, w_up, False)
            hidden = activate(keep, got)
            other = swap(hidden)
            return lower(hidden, other, w_down, inner)
        data = jnp.concatenate(rows, axis=0)
        gate_part = jnp.dot(data, w_gate, preferred_element_type=F32)
        up_part = jnp.dot(data, w_up, preferred_element_type=F32)
        gate_sum = lax.psum_scatter(gate_part, "tp", scatter_dimension=1, tiled=True)
        up_sum = lax.psum_scatter(up_part, "tp", scatter_dimension=1, tiled=True)
        hidden = (jax.nn.silu(gate_sum) * up_sum).astype(BF16)
        hidden = lax.all_gather(hidden, "tp", axis=1, tiled=True)
        out = jnp.dot(hidden, w_down, preferred_element_type=F32).astype(BF16)
        return jnp.split(out, inner, axis=0)

    def gather(rows, mix, partials, kind=BF16):
        returned = near(rows)
        return combine(returned, mix, partials, kind)

    own = stage(tokens, routes, gate_levels)
    if outer != 4:
        sent = [send([own])]
        sent += [send([flip(own, k)]) for k in range(1, outer)]
        partials = []
        for k in range(1, outer):
            mix, rows = sent[k]
            part = gather(expert(rows, w_gate, w_up, w_down), mix, [])
            partials.append(flip(part, k))
        mix, rows = sent[0]
        return gather(expert(rows, w_gate, w_up, w_down), mix, partials)

    beside = flip(own, 1)
    across = hop(own, [(1, 2), (2, 1)])
    mix0, rows0 = send([own])
    relayed = hop(beside, [(1, 2), (2, 1)])
    outward = hop(across, [(1, 0), (2, 3)])
    mix1, rows1 = send([beside])
    last = hop(relayed, [(1, 0), (2, 3)])
    mix2, rows2 = send([relayed, outward])
    mix3, rows3 = send([across, last])
    weights = [load(w_gate), load(w_up), load(w_down)]
    made = [expert(rows, *weights) for rows in (rows0, rows1, rows2, rows3)]
    passed = flip(gather(made[2], mix2, []), 1)
    distant = flip(gather(made[3], mix3, [passed]), 3)
    close = flip(gather(made[1], mix1, []), 1)
    return gather(made[0], mix0, [close, distant])


def solution(mesh):
    in_specs = (
        P("ep", "tp"),
        P("ep", None),
        P("ep", None),
        P("ep", "tp", None),
        P("ep", "tp", None),
        P("ep", None, "tp"),
    )
    return jax.shard_map(
        on_device, mesh=mesh, in_specs=in_specs, out_specs=P("ep", "tp"), check_vma=False
    )
```

profile of v0, /device:TPU:14, one launch (start us, length us, event | category | flops | bytes accessed | tf_op | source)
XLA Modules:
  0.0 149.1 jit_solution(13609621453170414890)
XLA Ops:
  0.0 1.1 stage.1.refs_0_
  1.1 0.5 collective-permute-start.8
  1.6 4.6 %collective-permute-start.18 = (bf16[128,1920]{1,0:T(8,128)(2,1)S(1)}, bf16[128,1920]{1,0:T(8,128)(2,1)S(1)}, u32[]{:S(2)}, u32[]{:S(2)}) collective-permute-start(bf16[128,1920]{1,0:T(8,128)(2,1)S(1)} %stage.1.refs_0_), channel_id=1, source_target_pairs={{8,16},{10,18},{12,20},{14,22},{16,8},{18,10},{20,12},{22,14},{9,1... | collective-permute-start | bytes 1474568 | tf_op jit(solution)/shard_map/ppermute | solution.py:289
  6.2 7.9 %collective-permute-done.8.refs_0_ = bf16[128,1920]{1,0:T(8,128)(2,1)S(1)} collective-permute-done((bf16[128,1920]{1,0:T(8,128)(2,1)S(1)}, bf16[128,1920]{1,0:T(8,128)(2,1)S(1)}, u32[]{:S(2)}, u32[]{:S(2)}) %collective-permute-start.8) | collective-permute-done | bytes 491552 | tf_op jit(solution)/shard_map/ppermute | solution.py:293
  14.1 3.5 %collective-permute-start.19 = (bf16[128,1920]{1,0:T(8,128)(2,1)S(1)}, bf16[128,1920]{1,0:T(8,128)(2,1)S(1)}, u32[]{:S(2)}, u32[]{:S(2)}) collective-permute-start(bf16[128,1920]{1,0:T(8,128)(2,1)S(1)} %collective-permute-done.8.refs_0_), channel_id=1, source_target_pairs={{8,16},{10,18},{12,20},{14,22},{16,8},{18,10},{20,12},{22,14},{9,1... | collective-permute-start | bytes 1474568 | tf_op jit(solution)/shard_map/ppermute | solution.py:289
  17.6 1.3 collective-permute-start.29
  18.9 9.2 %collective-permute-done.19.refs_0_ = bf16[128,1920]{1,0:T(8,128)(2,1)S(1)} collective-permute-done((bf16[128,1920]{1,0:T(8,128)(2,1)S(1)}, bf16[128,1920]{1,0:T(8,128)(2,1)S(1)}, u32[]{:S(2)}, u32[]{:S(2)}) %collective-permute-start.19) | collective-permute-done | bytes 491552 | tf_op jit(solution)/shard_map/ppermute | solution.py:289
  28.5 1.0 pack.7
  29.5 0.6 collective-permute-start.30
  30.1 0.5 collective-permute-start.31
  30.6 2.4 %collective-permute-start.32 = (bf16[72,1792]{1,0:T(8,128)(2,1)S(1)}, bf16[72,1792]{1,0:T(8,128)(2,1)S(1)}, u32[]{:S(2)}, u32[]{:S(2)}) collective-permute-start(bf16[72,1792]{1,0:T(8,128)(2,1)S(1)} %get-tuple-element.72), channel_id=1, source_target_pairs={{0,6},{2,4},{4,2},{6,0},{8,14},{10,12},{12,10},{14,8},{16,22},{18,... | collective-permute-start | bytes 774152 | tf_op jit(solution)/shard_map/ppermute | solution.py:298
  33.1 4.4 %collective-permute-start.20 = (bf16[128,1920]{1,0:T(8,128)(2,1)S(1)}, bf16[128,1920]{1,0:T(8,128)(2,1)S(1)}, u32[]{:S(2)}, u32[]{:S(2)}) collective-permute-start(bf16[128,1920]{1,0:T(8,128)(2,1)S(1)} %collective-permute-done.19.refs_0_), channel_id=1, source_target_pairs={{8,0},{10,2},{12,4},{14,6},{16,24},{18,26},{20,28},{22,30},{9,1},{... | collective-permute-start | bytes 1474568 | tf_op jit(solution)/shard_map/ppermute | solution.py:289
  37.5 1.0 pack.5
  38.5 0.6 collective-permute-start.10
  39.1 1.5 %collective-permute-start.11 = (bf16[72,1792]{1,0:T(8,128)(2,1)S(1)}, bf16[72,1792]{1,0:T(8,128)(2,1)S(1)}, u32[]{:S(2)}, u32[]{:S(2)}) collective-permute-start(bf16[72,1792]{1,0:T(8,128)(2,1)S(1)} %get-tuple-element.54), channel_id=1, source_target_pairs={{0,6},{2,4},{4,2},{6,0},{8,14},{10,12},{12,10},{14,8},{16,22},{18,... | collective-permute-start | bytes 774152 | tf_op jit(solution)/shard_map/ppermute | solution.py:298
  40.6 5.6 %collective-permute-done.31.refs_2_ = bf16[72,1792]{1,0:T(8,128)(2,1)S(1)} collective-permute-done((bf16[72,1792]{1,0:T(8,128)(2,1)S(1)}, bf16[72,1792]{1,0:T(8,128)(2,1)S(1)}, u32[]{:S(2)}, u32[]{:S(2)}) %collective-permute-start.31) | collective-permute-done | bytes 258080 | tf_op jit(solution)/shard_map/ppermute | solution.py:298
  46.3 3.9 %collective-permute-start.9 = (bf16[72,1792]{1,0:T(8,128)(2,1)S(1)}, bf16[72,1792]{1,0:T(8,128)(2,1)S(1)}, u32[]{:S(2)}, u32[]{:S(2)}) collective-permute-start(bf16[72,1792]{1,0:T(8,128)(2,1)S(1)} %get-tuple-element.52), channel_id=1, source_target_pairs={{0,2},{2,0},{4,6},{6,4},{8,10},{10,8},{12,14},{14,12},{16,18},{18,... | collective-permute-start | bytes 774152 | tf_op jit(solution)/shard_map/ppermute | solution.py:298
  50.1 2.0 %load.3.refs_4_ = bf16[1792,1024]{1,0:T(8,128)(2,1)S(1)} custom-call(bf16[1792,1024]{1,0:T(8,128)(2,1)} %bitcast.5), custom_call_target="tpu_custom_call" | custom-call | tf_op jit(solution)/shard_map/load/pallas_call | solution.py:58
  52.2 2.0 %load.4.refs_5_ = bf16[1792,1024]{1,0:T(8,128)(2,1)S(1)} custom-call(bf16[1792,1024]{1,0:T(8,128)(2,1)} %bitcast.6), custom_call_target="tpu_custom_call" | custom-call | tf_op jit(solution)/shard_map/load/pallas_call | solution.py:58
  54.3 1.3 lift.15
  55.6 1.3 lift.11
  56.9 0.6 collective-permute-start.12
  57.5 1.0 pack.6
  58.5 0.4 collective-permute-start.21
  58.9 3.1 %collective-permute-start.23 = (bf16[72,1792]{1,0:T(8,128)(2,1)S(1)}, bf16[72,1792]{1,0:T(8,128)(2,1)S(1)}, u32[]{:S(2)}, u32[]{:S(2)}) collective-permute-start(bf16[72,1792]{1,0:T(8,128)(2,1)S(1)} %get-tuple-element.63), channel_id=1, source_target_pairs={{0,6},{2,4},{4,2},{6,0},{8,14},{10,12},{12,10},{14,8},{16,22},{18,... | collective-permute-start | bytes 774152 | tf_op jit(solution)/shard_map/ppermute | solution.py:298
  62.1 1.0 pack.4
  63.1 4.6 %collective-permute-done.21.refs_1_ = bf16[72,1792]{1,0:T(8,128)(2,1)S(1)} collective-permute-done((bf16[72,1792]{1,0:T(8,128)(2,1)S(1)}, bf16[72,1792]{1,0:T(8,128)(2,1)S(1)}, u32[]{:S(2)}, u32[]{:S(2)}) %collective-permute-start.21) | collective-permute-done | bytes 258080 | tf_op jit(solution)/shard_map/ppermute | solution.py:298
  68.0 4.8 %collective-permute-done.22.refs_2_ = bf16[72,1792]{1,0:T(8,128)(2,1)S(1)} collective-permute-done((bf16[72,1792]{1,0:T(8,128)(2,1)S(1)}, bf16[72,1792]{1,0:T(8,128)(2,1)S(1)}, u32[]{:S(2)}, u32[]{:S(2)}) %collective-permute-start.22) | collective-permute-done | bytes 258080 | tf_op jit(solution)/shard_map/ppermute | solution.py:298
  72.8 2.7 %collective-permute-start.2 = (bf16[72,1792]{1,0:T(8,128)(2,1)S(1)}, bf16[72,1792]{1,0:T(8,128)(2,1)S(1)}, u32[]{:S(2)}, u32[]{:S(2)}) collective-permute-start(bf16[72,1792]{1,0:T(8,128)(2,1)S(1)} %get-tuple-element.45), channel_id=1, source_target_pairs={{0,6},{2,4},{4,2},{6,0},{8,14},{10,12},{12,10},{14,8},{16,22},{18,... | collective-permute-start | bytes 774152 | tf_op jit(solution)/shard_map/ppermute | solution.py:298
  75.5 1.3 lift.13
  76.8 1.3 lift.14.keep_ref
  78.3 0.6 collective-permute-start.34
  78.9 2.0 %load.5.w_ref = bf16[1024,1792]{1,0:T(8,128)(2,1)S(1)} custom-call(bf16[1024,1792]{1,0:T(8,128)(2,1)} %bitcast.7), custom_call_target="tpu_custom_call" | custom-call | tf_op jit(solution)/shard_map/load/pallas_call | solution.py:58
  80.9 1.3 lift.10.keep_ref
  82.5 3.2 %collective-permute-done.1.refs_2_ = bf16[72,1792]{1,0:T(8,128)(2,1)S(1)} collective-permute-done((bf16[72,1792]{1,0:T(8,128)(2,1)S(1)}, bf16[72,1792]{1,0:T(8,128)(2,1)S(1)}, u32[]{:S(2)}, u32[]{:S(2)}) %collective-permute-start.1) | collective-permute-done | bytes 258080 | tf_op jit(solution)/shard_map/ppermute | solution.py:298
  85.7 1.3 lift.9
  87.1 1.2 lower.7
  88.3 0.9 collective-permute-start.35
  89.5 1.2 lift.12.keep_ref
  91.1 2.4 %collective-permute-start.37 = (bf16[72,1792]{1,0:T(8,128)(2,1)S(1)}, bf16[72,1792]{1,0:T(8,128)(2,1)S(1)}, u32[]{:S(2)}, u32[]{:S(2)}) collective-permute-start(bf16[72,1792]{1,0:T(8,128)(2,1)S(1)} %get-tuple-element.76), channel_id=1, source_target_pairs={{0,6},{2,4},{4,2},{6,0},{8,14},{10,12},{12,10},{14,8},{16,22},{18,... | collective-permute-start | bytes 774152 | tf_op jit(solution)/shard_map/ppermute | solution.py:298
  93.5 1.2 lower.5
  94.7 2.7 %collective-permute-done.35.refs_1_ = bf16[72,1792]{1,0:T(8,128)(2,1)S(1)} collective-permute-done((bf16[72,1792]{1,0:T(8,128)(2,1)S(1)}, bf16[72,1792]{1,0:T(8,128)(2,1)S(1)}, u32[]{:S(2)}, u32[]{:S(2)}) %collective-permute-start.35) | collective-permute-done | bytes 258080 | tf_op jit(solution)/shard_map/ppermute | solution.py:298
  97.5 0.8 collective-permute-start.14
  98.3 5.5 %collective-permute-done.36.refs_2_ = bf16[72,1792]{1,0:T(8,128)(2,1)S(1)} collective-permute-done((bf16[72,1792]{1,0:T(8,128)(2,1)S(1)}, bf16[72,1792]{1,0:T(8,128)(2,1)S(1)}, u32[]{:S(2)}, u32[]{:S(2)}) %collective-permute-start.36) | collective-permute-done | bytes 258080 | tf_op jit(solution)/shard_map/ppermute | solution.py:298
  103.8 0.8 combine.5
  104.6 2.7 %collective-permute-start.38 = (bf16[128,1792]{1,0:T(8,128)(2,1)S(1)}, bf16[128,1792]{1,0:T(8,128)(2,1)S(1)}, u32[]{:S(2)}, u32[]{:S(2)}) collective-permute-start(bf16[128,1792]{1,0:T(8,128)(2,1)S(1)} %combine.5), channel_id=1, source_target_pairs={{0,8},{2,10},{4,12},{6,14},{8,0},{10,2},{12,4},{14,6},{16,24},{18,... | collective-permute-start | bytes 1376264 | tf_op jit(solution)/shard_map/ppermute | solution.py:293
  107.2 2.6 %collective-permute-start.16 = (bf16[72,1792]{1,0:T(8,128)(2,1)S(1)}, bf16[72,1792]{1,0:T(8,128)(2,1)S(1)}, u32[]{:S(2)}, u32[]{:S(2)}) collective-permute-start(bf16[72,1792]{1,0:T(8,128)(2,1)S(1)} %get-tuple-element.58), channel_id=1, source_target_pairs={{0,6},{2,4},{4,2},{6,0},{8,14},{10,12},{12,10},{14,8},{16,22},{18,... | collective-permute-start | bytes 774152 | tf_op jit(solution)/shard_map/ppermute | solution.py:298
  109.9 1.2 lower.6
  111.1 0.9 collective-permute-start.26
  112.0 2.4 %collective-permute-done.15.refs_2_ = bf16[72,1792]{1,0:T(8,128)(2,1)S(1)} collective-permute-done((bf16[72,1792]{1,0:T(8,128)(2,1)S(1)}, bf16[72,1792]{1,0:T(8,128)(2,1)S(1)}, u32[]{:S(2)}, u32[]{:S(2)}) %collective-permute-start.15) | collective-permute-done | bytes 258080 | tf_op jit(solution)/shard_map/ppermute | solution.py:298
  114.4 2.1 %collective-permute-start.28 = (bf16[72,1792]{1,0:T(8,128)(2,1)S(1)}, bf16[72,1792]{1,0:T(8,128)(2,1)S(1)}, u32[]{:S(2)}, u32[]{:S(2)}) collective-permute-start(bf16[72,1792]{1,0:T(8,128)(2,1)S(1)} %get-tuple-element.67), channel_id=1, source_target_pairs={{0,6},{2,4},{4,2},{6,0},{8,14},{10,12},{12,10},{14,8},{16,22},{18,... | collective-permute-start | bytes 774152 | tf_op jit(solution)/shard_map/ppermute | solution.py:298
  116.5 1.2 lift.8.keep_ref
  118.1 0.6 combine.4
  118.8 4.5 %collective-permute-start.17 = (bf16[128,1792]{1,0:T(8,128)(2,1)S(1)}, bf16[128,1792]{1,0:T(8,128)(2,1)S(1)}, u32[]{:S(2)}, u32[]{:S(2)}) collective-permute-start(bf16[128,1792]{1,0:T(8,128)(2,1)S(1)} %combine.4), channel_id=1, source_target_pairs={{0,8},{2,10},{4,12},{6,14},{8,0},{10,2},{12,4},{14,6},{16,24},{18,... | collective-permute-start | bytes 1376264 | tf_op jit(solution)/shard_map/ppermute | solution.py:293
  123.3 3.3 %collective-permute-done.27.refs_2_ = bf16[72,1792]{1,0:T(8,128)(2,1)S(1)} collective-permute-done((bf16[72,1792]{1,0:T(8,128)(2,1)S(1)}, bf16[72,1792]{1,0:T(8,128)(2,1)S(1)}, u32[]{:S(2)}, u32[]{:S(2)}) %collective-permute-start.27) | collective-permute-done | bytes 258080 | tf_op jit(solution)/shard_map/ppermute | solution.py:298
  126.7 0.6 combine.6
  127.3 1.3 collective-permute-start.39
  128.7 1.2 lower.4
  129.9 1.6 %collective-permute-start.5 = (bf16[72,1792]{1,0:T(8,128)(2,1)S(1)}, bf16[72,1792]{1,0:T(8,128)(2,1)S(1)}, u32[]{:S(2)}, u32[]{:S(2)}) collective-permute-start(bf16[72,1792]{1,0:T(8,128)(2,1)S(1)} %get-tuple-element.47), channel_id=1, source_target_pairs={{0,2},{2,0},{4,6},{6,4},{8,10},{10,8},{12,14},{14,12},{16,18},{18,... | collective-permute-start | bytes 774152 | tf_op jit(solution)/shard_map/ppermute | solution.py:298
  131.8 1.7 %collective-permute-start.7 = (bf16[72,1792]{1,0:T(8,128)(2,1)S(1)}, bf16[72,1792]{1,0:T(8,128)(2,1)S(1)}, u32[]{:S(2)}, u32[]{:S(2)}) collective-permute-start(bf16[72,1792]{1,0:T(8,128)(2,1)S(1)} %get-tuple-element.49), channel_id=1, source_target_pairs={{0,6},{2,4},{4,2},{6,0},{8,14},{10,12},{12,10},{14,8},{16,22},{18,... | collective-permute-start | bytes 774152 | tf_op jit(solution)/shard_map/ppermute | solution.py:298
  133.5 5.1 %collective-permute-done.5.refs_1_ = bf16[72,1792]{1,0:T(8,128)(2,1)S(1)} collective-permute-done((bf16[72,1792]{1,0:T(8,128)(2,1)S(1)}, bf16[72,1792]{1,0:T(8,128)(2,1)S(1)}, u32[]{:S(2)}, u32[]{:S(2)}) %collective-permute-start.5) | collective-permute-done | bytes 258080 | tf_op jit(solution)/shard_map/ppermute | solution.py:298
  138.6 3.9 %collective-permute-done.6.refs_2_ = bf16[72,1792]{1,0:T(8,128)(2,1)S(1)} collective-permute-done((bf16[72,1792]{1,0:T(8,128)(2,1)S(1)}, bf16[72,1792]{1,0:T(8,128)(2,1)S(1)}, u32[]{:S(2)}, u32[]{:S(2)}) %collective-permute-start.6) | collective-permute-done | bytes 258080 | tf_op jit(solution)/shard_map/ppermute | solution.py:298
  142.5 5.2 %collective-permute-done.39.refs_5_ = bf16[128,1792]{1,0:T(8,128)(2,1)S(1)} collective-permute-done((bf16[128,1792]{1,0:T(8,128)(2,1)S(1)}, bf16[128,1792]{1,0:T(8,128)(2,1)S(1)}, u32[]{:S(2)}, u32[]{:S(2)}) %collective-permute-start.39) | collective-permute-done | bytes 458784 | tf_op jit(solution)/shard_map/ppermute | solution.py:293
  147.7 1.4 combine.7
  (44 shorter events, 2.9 us)
Async XLA Ops:
  1.1 13.0 %collective-permute-start.8 = (bf16[128,1920]{1,0:T(8,128)(2,1)S(1)}, bf16[128,1920]{1,0:T(8,128)(2,1)S(1)}, u32[]{:S(2)}, u32[]{:S(2)}) collective-permute-start(bf16[128,1920]{1,0:T(8,128)(2,1)S(1)} %stage.1.refs_0_), channel_id=1, source_target_pairs={{0,8},{2,10},{4,12},{6,14},{8,0},{10,2},{12,4},{14,6},{16,24},{18,... | collective-permute-start | bytes 1474568 | tf_op jit(solution)/shard_map/ppermute | solution.py:293
  1.6 16.0 %collective-permute-start.18 = (bf16[128,1920]{1,0:T(8,128)(2,1)S(1)}, bf16[128,1920]{1,0:T(8,128)(2,1)S(1)}, u32[]{:S(2)}, u32[]{:S(2)}) collective-permute-start(bf16[128,1920]{1,0:T(8,128)(2,1)S(1)} %stage.1.refs_0_), channel_id=1, source_target_pairs={{8,16},{10,18},{12,20},{14,22},{16,8},{18,10},{20,12},{22,14},{9,1... | collective-permute-start | bytes 1474568 | tf_op jit(solution)/shard_map/ppermute | solution.py:289
  14.1 14.0 %collective-permute-start.19 = (bf16[128,1920]{1,0:T(8,128)(2,1)S(1)}, bf16[128,1920]{1,0:T(8,128)(2,1)S(1)}, u32[]{:S(2)}, u32[]{:S(2)}) collective-permute-start(bf16[128,1920]{1,0:T(8,128)(2,1)S(1)} %collective-permute-done.8.refs_0_), channel_id=1, source_target_pairs={{8,16},{10,18},{12,20},{14,22},{16,8},{18,10},{20,12},{22,14},{9,1... | collective-permute-start | bytes 1474568 | tf_op jit(solution)/shard_map/ppermute | solution.py:289
  17.6 10.9 %collective-permute-start.29 = (bf16[128,1920]{1,0:T(8,128)(2,1)S(1)}, bf16[128,1920]{1,0:T(8,128)(2,1)S(1)}, u32[]{:S(2)}, u32[]{:S(2)}) collective-permute-start(bf16[128,1920]{1,0:T(8,128)(2,1)S(1)} %collective-permute-done.18.refs_0_), channel_id=1, source_target_pairs={{8,0},{10,2},{12,4},{14,6},{16,24},{18,26},{20,28},{22,30},{9,1},{... | collective-permute-start | bytes 1474568 | tf_op jit(solution)/shard_map/ppermute | solution.py:289
  29.5 9.6 %collective-permute-start.30 = (bf16[72,1792]{1,0:T(8,128)(2,1)S(1)}, bf16[72,1792]{1,0:T(8,128)(2,1)S(1)}, u32[]{:S(2)}, u32[]{:S(2)}) collective-permute-start(bf16[72,1792]{1,0:T(8,128)(2,1)S(1)} %get-tuple-element.70), channel_id=1, source_target_pairs={{0,2},{2,0},{4,6},{6,4},{8,10},{10,8},{12,14},{14,12},{16,18},{18,... | collective-permute-start | bytes 774152 | tf_op jit(solution)/shard_map/ppermute | solution.py:298
  30.1 16.1 %collective-permute-start.31 = (bf16[72,1792]{1,0:T(8,128)(2,1)S(1)}, bf16[72,1792]{1,0:T(8,128)(2,1)S(1)}, u32[]{:S(2)}, u32[]{:S(2)}) collective-permute-start(bf16[72,1792]{1,0:T(8,128)(2,1)S(1)} %get-tuple-element.71), channel_id=1, source_target_pairs={{0,4},{2,6},{4,0},{6,2},{8,12},{10,14},{12,8},{14,10},{16,20},{18,... | collective-permute-start | bytes 774152 | tf_op jit(solution)/shard_map/ppermute | solution.py:298
  30.6 23.6 %collective-permute-start.32 = (bf16[72,1792]{1,0:T(8,128)(2,1)S(1)}, bf16[72,1792]{1,0:T(8,128)(2,1)S(1)}, u32[]{:S(2)}, u32[]{:S(2)}) collective-permute-start(bf16[72,1792]{1,0:T(8,128)(2,1)S(1)} %get-tuple-element.72), channel_id=1, source_target_pairs={{0,6},{2,4},{4,2},{6,0},{8,14},{10,12},{12,10},{14,8},{16,22},{18,... | collective-permute-start | bytes 774152 | tf_op jit(solution)/shard_map/ppermute | solution.py:298
  33.1 24.4 %collective-permute-start.20 = (bf16[128,1920]{1,0:T(8,128)(2,1)S(1)}, bf16[128,1920]{1,0:T(8,128)(2,1)S(1)}, u32[]{:S(2)}, u32[]{:S(2)}) collective-permute-start(bf16[128,1920]{1,0:T(8,128)(2,1)S(1)} %collective-permute-done.19.refs_0_), channel_id=1, source_target_pairs={{8,0},{10,2},{12,4},{14,6},{16,24},{18,26},{20,28},{22,30},{9,1},{... | collective-permute-start | bytes 1474568 | tf_op jit(solution)/shard_map/ppermute | solution.py:289
  38.5 17.1 %collective-permute-start.10 = (bf16[72,1792]{1,0:T(8,128)(2,1)S(1)}, bf16[72,1792]{1,0:T(8,128)(2,1)S(1)}, u32[]{:S(2)}, u32[]{:S(2)}) collective-permute-start(bf16[72,1792]{1,0:T(8,128)(2,1)S(1)} %get-tuple-element.53), channel_id=1, source_target_pairs={{0,4},{2,6},{4,0},{6,2},{8,12},{10,14},{12,8},{14,10},{16,20},{18,... | collective-permute-start | bytes 774152 | tf_op jit(solution)/shard_map/ppermute | solution.py:298
  39.1 16.5 %collective-permute-start.11 = (bf16[72,1792]{1,0:T(8,128)(2,1)S(1)}, bf16[72,1792]{1,0:T(8,128)(2,1)S(1)}, u32[]{:S(2)}, u32[]{:S(2)}) collective-permute-start(bf16[72,1792]{1,0:T(8,128)(2,1)S(1)} %get-tuple-element.54), channel_id=1, source_target_pairs={{0,6},{2,4},{4,2},{6,0},{8,14},{10,12},{12,10},{14,8},{16,22},{18,... | collective-permute-start | bytes 774152 | tf_op jit(solution)/shard_map/ppermute | solution.py:298
  46.3 9.4 %collective-permute-start.9 = (bf16[72,1792]{1,0:T(8,128)(2,1)S(1)}, bf16[72,1792]{1,0:T(8,128)(2,1)S(1)}, u32[]{:S(2)}, u32[]{:S(2)}) collective-permute-start(bf16[72,1792]{1,0:T(8,128)(2,1)S(1)} %get-tuple-element.52), channel_id=1, source_target_pairs={{0,2},{2,0},{4,6},{6,4},{8,10},{10,8},{12,14},{14,12},{16,18},{18,... | collective-permute-start | bytes 774152 | tf_op jit(solution)/shard_map/ppermute | solution.py:298
  55.5 21.2 %collective-permute-start.33 = (bf16[288,1024]{1,0:T(8,128)(2,1)S(1)}, bf16[288,1024]{1,0:T(8,128)(2,1)S(1)}, u32[]{:S(2)}, u32[]{:S(2)}) collective-permute-start(bf16[288,1024]{1,0:T(8,128)(2,1)S(1)} %lift.15), channel_id=1, source_target_pairs={{0,1},{1,0},{2,3},{3,2},{4,5},{5,4},{6,7},{7,6},{8,9},{9,8},{10,11... | collective-permute-start | bytes 1769480 | tf_op jit(solution)/shard_map/ppermute | solution.py:302
  56.9 21.4 %collective-permute-start.12 = (bf16[288,1024]{1,0:T(8,128)(2,1)S(1)}, bf16[288,1024]{1,0:T(8,128)(2,1)S(1)}, u32[]{:S(2)}, u32[]{:S(2)}) collective-permute-start(bf16[288,1024]{1,0:T(8,128)(2,1)S(1)} %lift.11), channel_id=1, source_target_pairs={{0,1},{1,0},{2,3},{3,2},{4,5},{5,4},{6,7},{7,6},{8,9},{9,8},{10,11... | collective-permute-start | bytes 1769480 | tf_op jit(solution)/shard_map/ppermute | solution.py:302
  58.5 9.2 %collective-permute-start.21 = (bf16[72,1792]{1,0:T(8,128)(2,1)S(1)}, bf16[72,1792]{1,0:T(8,128)(2,1)S(1)}, u32[]{:S(2)}, u32[]{:S(2)}) collective-permute-start(bf16[72,1792]{1,0:T(8,128)(2,1)S(1)} %get-tuple-element.61), channel_id=1, source_target_pairs={{0,2},{2,0},{4,6},{6,4},{8,10},{10,8},{12,14},{14,12},{16,18},{18,... | collective-permute-start | bytes 774152 | tf_op jit(solution)/shard_map/ppermute | solution.py:298
  58.9 13.9 %collective-permute-start.22 = (bf16[72,1792]{1,0:T(8,128)(2,1)S(1)}, bf16[72,1792]{1,0:T(8,128)(2,1)S(1)}, u32[]{:S(2)}, u32[]{:S(2)}) collective-permute-start(bf16[72,1792]{1,0:T(8,128)(2,1)S(1)} %get-tuple-element.62), channel_id=1, source_target_pairs={{0,4},{2,6},{4,0},{6,2},{8,12},{10,14},{12,8},{14,10},{16,20},{18,... | collective-permute-start | bytes 774152 | tf_op jit(solution)/shard_map/ppermute | solution.py:298
  58.9 13.9 %collective-permute-start.23 = (bf16[72,1792]{1,0:T(8,128)(2,1)S(1)}, bf16[72,1792]{1,0:T(8,128)(2,1)S(1)}, u32[]{:S(2)}, u32[]{:S(2)}) collective-permute-start(bf16[72,1792]{1,0:T(8,128)(2,1)S(1)} %get-tuple-element.63), channel_id=1, source_target_pairs={{0,6},{2,4},{4,2},{6,0},{8,14},{10,12},{12,10},{14,8},{16,22},{18,... | collective-permute-start | bytes 774152 | tf_op jit(solution)/shard_map/ppermute | solution.py:298
  67.7 14.8 %collective-permute-start = (bf16[72,1792]{1,0:T(8,128)(2,1)S(1)}, bf16[72,1792]{1,0:T(8,128)(2,1)S(1)}, u32[]{:S(2)}, u32[]{:S(2)}) collective-permute-start(bf16[72,1792]{1,0:T(8,128)(2,1)S(1)} %get-tuple-element.43), channel_id=1, source_target_pairs={{0,2},{2,0},{4,6},{6,4},{8,10},{10,8},{12,14},{14,12},{16,18},{18,... | collective-permute-start | bytes 774152 | tf_op jit(solution)/shard_map/ppermute | solution.py:298
  72.8 12.9 %collective-permute-start.1 = (bf16[72,1792]{1,0:T(8,128)(2,1)S(1)}, bf16[72,1792]{1,0:T(8,128)(2,1)S(1)}, u32[]{:S(2)}, u32[]{:S(2)}) collective-permute-start(bf16[72,1792]{1,0:T(8,128)(2,1)S(1)} %get-tuple-element.44), channel_id=1, source_target_pairs={{0,4},{2,6},{4,0},{6,2},{8,12},{10,14},{12,8},{14,10},{16,20},{18,... | collective-permute-start | bytes 774152 | tf_op jit(solution)/shard_map/ppermute | solution.py:298
  72.8 12.9 %collective-permute-start.2 = (bf16[72,1792]{1,0:T(8,128)(2,1)S(1)}, bf16[72,1792]{1,0:T(8,128)(2,1)S(1)}, u32[]{:S(2)}, u32[]{:S(2)}) collective-permute-start(bf16[72,1792]{1,0:T(8,128)(2,1)S(1)} %get-tuple-element.45), channel_id=1, source_target_pairs={{0,6},{2,4},{4,2},{6,0},{8,14},{10,12},{12,10},{14,8},{16,22},{18,... | collective-permute-start | bytes 774152 | tf_op jit(solution)/shard_map/ppermute | solution.py:298
  76.7 14.0 %collective-permute-start.24 = (bf16[288,1024]{1,0:T(8,128)(2,1)S(1)}, bf16[288,1024]{1,0:T(8,128)(2,1)S(1)}, u32[]{:S(2)}, u32[]{:S(2)}) collective-permute-start(bf16[288,1024]{1,0:T(8,128)(2,1)S(1)} %lift.13), channel_id=1, source_target_pairs={{0,1},{1,0},{2,3},{3,2},{4,5},{5,4},{6,7},{7,6},{8,9},{9,8},{10,11... | collective-permute-start | bytes 1769480 | tf_op jit(solution)/shard_map/ppermute | solution.py:302
  78.3 8.7 %collective-permute-start.34 = (bf16[288,512]{1,0:T(8,128)(2,1)S(1)}, bf16[288,512]{1,0:T(8,128)(2,1)S(1)}, u32[]{:S(2)}, u32[]{:S(2)}) collective-permute-start(bf16[288,512]{1,0:T(8,128)(2,1)S(1)} %activate.7.own_ref), channel_id=1, source_target_pairs={{0,1},{1,0},{2,3},{3,2},{4,5},{5,4},{6,7},{7,6},{8,9},{9,8},{10,11... | collective-permute-start | bytes 884744 | tf_op jit(solution)/shard_map/ppermute | solution.py:302
  82.5 8.6 %collective-permute-start.13 = (bf16[288,512]{1,0:T(8,128)(2,1)S(1)}, bf16[288,512]{1,0:T(8,128)(2,1)S(1)}, u32[]{:S(2)}, u32[]{:S(2)}) collective-permute-start(bf16[288,512]{1,0:T(8,128)(2,1)S(1)} %activate.5.own_ref), channel_id=1, source_target_pairs={{0,1},{1,0},{2,3},{3,2},{4,5},{5,4},{6,7},{7,6},{8,9},{9,8},{10,11... | collective-permute-start | bytes 884744 | tf_op jit(solution)/shard_map/ppermute | solution.py:302
  87.0 24.1 %collective-permute-start.3 = (bf16[288,1024]{1,0:T(8,128)(2,1)S(1)}, bf16[288,1024]{1,0:T(8,128)(2,1)S(1)}, u32[]{:S(2)}, u32[]{:S(2)}) collective-permute-start(bf16[288,1024]{1,0:T(8,128)(2,1)S(1)} %lift.9), channel_id=1, source_target_pairs={{0,1},{1,0},{2,3},{3,2},{4,5},{5,4},{6,7},{7,6},{8,9},{9,8},{10,11... | collective-permute-start | bytes 1769480 | tf_op jit(solution)/shard_map/ppermute | solution.py:302
  88.3 9.2 %collective-permute-start.35 = (bf16[72,1792]{1,0:T(8,128)(2,1)S(1)}, bf16[72,1792]{1,0:T(8,128)(2,1)S(1)}, u32[]{:S(2)}, u32[]{:S(2)}) collective-permute-start(bf16[72,1792]{1,0:T(8,128)(2,1)S(1)} %get-tuple-element.74), channel_id=1, source_target_pairs={{0,2},{2,0},{4,6},{6,4},{8,10},{10,8},{12,14},{14,12},{16,18},{18,... | collective-permute-start | bytes 774152 | tf_op jit(solution)/shard_map/ppermute | solution.py:298
  89.2 14.6 %collective-permute-start.36 = (bf16[72,1792]{1,0:T(8,128)(2,1)S(1)}, bf16[72,1792]{1,0:T(8,128)(2,1)S(1)}, u32[]{:S(2)}, u32[]{:S(2)}) collective-permute-start(bf16[72,1792]{1,0:T(8,128)(2,1)S(1)} %get-tuple-element.75), channel_id=1, source_target_pairs={{0,4},{2,6},{4,0},{6,2},{8,12},{10,14},{12,8},{14,10},{16,20},{18,... | collective-permute-start | bytes 774152 | tf_op jit(solution)/shard_map/ppermute | solution.py:298
  91.0 16.2 %collective-permute-start.25 = (bf16[288,512]{1,0:T(8,128)(2,1)S(1)}, bf16[288,512]{1,0:T(8,128)(2,1)S(1)}, u32[]{:S(2)}, u32[]{:S(2)}) collective-permute-start(bf16[288,512]{1,0:T(8,128)(2,1)S(1)} %activate.6.own_ref), channel_id=1, source_target_pairs={{0,1},{1,0},{2,3},{3,2},{4,5},{5,4},{6,7},{7,6},{8,9},{9,8},{10,11... | collective-permute-start | bytes 884744 | tf_op jit(solution)/shard_map/ppermute | solution.py:302
  91.1 12.7 %collective-permute-start.37 = (bf16[72,1792]{1,0:T(8,128)(2,1)S(1)}, bf16[72,1792]{1,0:T(8,128)(2,1)S(1)}, u32[]{:S(2)}, u32[]{:S(2)}) collective-permute-start(bf16[72,1792]{1,0:T(8,128)(2,1)S(1)} %get-tuple-element.76), channel_id=1, source_target_pairs={{0,6},{2,4},{4,2},{6,0},{8,14},{10,12},{12,10},{14,8},{16,22},{18,... | collective-permute-start | bytes 774152 | tf_op jit(solution)/shard_map/ppermute | solution.py:298
  97.5 14.6 %collective-permute-start.14 = (bf16[72,1792]{1,0:T(8,128)(2,1)S(1)}, bf16[72,1792]{1,0:T(8,128)(2,1)S(1)}, u32[]{:S(2)}, u32[]{:S(2)}) collective-permute-start(bf16[72,1792]{1,0:T(8,128)(2,1)S(1)} %get-tuple-element.56), channel_id=1, source_target_pairs={{0,2},{2,0},{4,6},{6,4},{8,10},{10,8},{12,14},{14,12},{16,18},{18,... | collective-permute-start | bytes 774152 | tf_op jit(solution)/shard_map/ppermute | solution.py:298
  103.8 10.7 %collective-permute-start.15 = (bf16[72,1792]{1,0:T(8,128)(2,1)S(1)}, bf16[72,1792]{1,0:T(8,128)(2,1)S(1)}, u32[]{:S(2)}, u32[]{:S(2)}) collective-permute-start(bf16[72,1792]{1,0:T(8,128)(2,1)S(1)} %get-tuple-element.57), channel_id=1, source_target_pairs={{0,4},{2,6},{4,0},{6,2},{8,12},{10,14},{12,8},{14,10},{16,20},{18,... | collective-permute-start | bytes 774152 | tf_op jit(solution)/shard_map/ppermute | solution.py:298
  104.6 14.2 %collective-permute-start.38 = (bf16[128,1792]{1,0:T(8,128)(2,1)S(1)}, bf16[128,1792]{1,0:T(8,128)(2,1)S(1)}, u32[]{:S(2)}, u32[]{:S(2)}) collective-permute-start(bf16[128,1792]{1,0:T(8,128)(2,1)S(1)} %combine.5), channel_id=1, source_target_pairs={{0,8},{2,10},{4,12},{6,14},{8,0},{10,2},{12,4},{14,6},{16,24},{18,... | collective-permute-start | bytes 1376264 | tf_op jit(solution)/shard_map/ppermute | solution.py:293
  107.2 10.8 %collective-permute-start.16 = (bf16[72,1792]{1,0:T(8,128)(2,1)S(1)}, bf16[72,1792]{1,0:T(8,128)(2,1)S(1)}, u32[]{:S(2)}, u32[]{:S(2)}) collective-permute-start(bf16[72,1792]{1,0:T(8,128)(2,1)S(1)} %get-tuple-element.58), channel_id=1, source_target_pairs={{0,6},{2,4},{4,2},{6,0},{8,14},{10,12},{12,10},{14,8},{16,22},{18,... | collective-permute-start | bytes 774152 | tf_op jit(solution)/shard_map/ppermute | solution.py:298
  111.1 12.2 %collective-permute-start.26 = (bf16[72,1792]{1,0:T(8,128)(2,1)S(1)}, bf16[72,1792]{1,0:T(8,128)(2,1)S(1)}, u32[]{:S(2)}, u32[]{:S(2)}) collective-permute-start(bf16[72,1792]{1,0:T(8,128)(2,1)S(1)} %get-tuple-element.65), channel_id=1, source_target_pairs={{0,2},{2,0},{4,6},{6,4},{8,10},{10,8},{12,14},{14,12},{16,18},{18,... | collective-permute-start | bytes 774152 | tf_op jit(solution)/shard_map/ppermute | solution.py:298
  112.0 14.6 %collective-permute-start.27 = (bf16[72,1792]{1,0:T(8,128)(2,1)S(1)}, bf16[72,1792]{1,0:T(8,128)(2,1)S(1)}, u32[]{:S(2)}, u32[]{:S(2)}) collective-permute-start(bf16[72,1792]{1,0:T(8,128)(2,1)S(1)} %get-tuple-element.66), channel_id=1, source_target_pairs={{0,4},{2,6},{4,0},{6,2},{8,12},{10,14},{12,8},{14,10},{16,20},{18,... | collective-permute-start | bytes 774152 | tf_op jit(solution)/shard_map/ppermute | solution.py:298
  114.4 12.3 %collective-permute-start.28 = (bf16[72,1792]{1,0:T(8,128)(2,1)S(1)}, bf16[72,1792]{1,0:T(8,128)(2,1)S(1)}, u32[]{:S(2)}, u32[]{:S(2)}) collective-permute-start(bf16[72,1792]{1,0:T(8,128)(2,1)S(1)} %get-tuple-element.67), channel_id=1, source_target_pairs={{0,6},{2,4},{4,2},{6,0},{8,14},{10,12},{12,10},{14,8},{16,22},{18,... | collective-permute-start | bytes 774152 | tf_op jit(solution)/shard_map/ppermute | solution.py:298
  118.0 10.6 %collective-permute-start.4 = (bf16[288,512]{1,0:T(8,128)(2,1)S(1)}, bf16[288,512]{1,0:T(8,128)(2,1)S(1)}, u32[]{:S(2)}, u32[]{:S(2)}) collective-permute-start(bf16[288,512]{1,0:T(8,128)(2,1)S(1)} %activate.4.own_ref), channel_id=1, source_target_pairs={{0,1},{1,0},{2,3},{3,2},{4,5},{5,4},{6,7},{7,6},{8,9},{9,8},{10,11... | collective-permute-start | bytes 884744 | tf_op jit(solution)/shard_map/ppermute | solution.py:302
  118.8 23.7 %collective-permute-start.17 = (bf16[128,1792]{1,0:T(8,128)(2,1)S(1)}, bf16[128,1792]{1,0:T(8,128)(2,1)S(1)}, u32[]{:S(2)}, u32[]{:S(2)}) collective-permute-start(bf16[128,1792]{1,0:T(8,128)(2,1)S(1)} %combine.4), channel_id=1, source_target_pairs={{0,8},{2,10},{4,12},{6,14},{8,0},{10,2},{12,4},{14,6},{16,24},{18,... | collective-permute-start | bytes 1376264 | tf_op jit(solution)/shard_map/ppermute | solution.py:293
  127.3 20.4 %collective-permute-start.39 = (bf16[128,1792]{1,0:T(8,128)(2,1)S(1)}, bf16[128,1792]{1,0:T(8,128)(2,1)S(1)}, u32[]{:S(2)}, u32[]{:S(2)}) collective-permute-start(bf16[128,1792]{1,0:T(8,128)(2,1)S(1)} %combine.6), channel_id=1, source_target_pairs={{0,24},{2,26},{4,28},{6,30},{8,16},{10,18},{12,20},{14,22},{16,8},... | collective-permute-start | bytes 1376264 | tf_op jit(solution)/shard_map/ppermute | solution.py:293
  129.9 8.7 %collective-permute-start.5 = (bf16[72,1792]{1,0:T(8,128)(2,1)S(1)}, bf16[72,1792]{1,0:T(8,128)(2,1)S(1)}, u32[]{:S(2)}, u32[]{:S(2)}) collective-permute-start(bf16[72,1792]{1,0:T(8,128)(2,1)S(1)} %get-tuple-element.47), channel_id=1, source_target_pairs={{0,2},{2,0},{4,6},{6,4},{8,10},{10,8},{12,14},{14,12},{16,18},{18,... | collective-permute-start | bytes 774152 | tf_op jit(solution)/shard_map/ppermute | solution.py:298
  131.5 11.0 %collective-permute-start.6 = (bf16[72,1792]{1,0:T(8,128)(2,1)S(1)}, bf16[72,1792]{1,0:T(8,128)(2,1)S(1)}, u32[]{:S(2)}, u32[]{:S(2)}) collective-permute-start(bf16[72,1792]{1,0:T(8,128)(2,1)S(1)} %get-tuple-element.48), channel_id=1, source_target_pairs={{0,4},{2,6},{4,0},{6,2},{8,12},{10,14},{12,8},{14,10},{16,20},{18,... | collective-permute-start | bytes 774152 | tf_op jit(solution)/shard_map/ppermute | solution.py:298
  131.8 10.7 %collective-permute-start.7 = (bf16[72,1792]{1,0:T(8,128)(2,1)S(1)}, bf16[72,1792]{1,0:T(8,128)(2,1)S(1)}, u32[]{:S(2)}, u32[]{:S(2)}) collective-permute-start(bf16[72,1792]{1,0:T(8,128)(2,1)S(1)} %get-tuple-element.49), channel_id=1, source_target_pairs={{0,6},{2,4},{4,2},{6,0},{8,14},{10,12},{12,10},{14,8},{16,22},{18,... | collective-permute-start | bytes 774152 | tf_op jit(solution)/shard_map/ppermute | solution.py:298
where the time goes:
time: 152 us; the launch traced here: 149 us
  waiting for transfers between devices  63.9 us (42%)
  starting transfers between devices  54.1 us (36%)
  Pallas kernels  30.7 us (20%)
    ppermute x24, waiting for transfers between devices, near(): lax.ppermute(rows[j], 'ep', [(i, i ^ j) for i in range(ep_count)])  41.1 us
    ppermute x24, starting transfers between devices, near(): lax.ppermute(rows[j], 'ep', [(i, i ^ j) for i in range(ep_count)])  29.8 us
    ppermute x4, starting transfers between devices, hop(): return lax.ppermute(value, 'ep', pairs)  13.8 us
    ppermute x4, waiting for transfers between devices, flip(): return lax.ppermute(value, 'ep', pairs)  13.1 us
    pallas_call x8, Pallas kernels, lift(): pl.pallas_call(body, out_shape=jax.ShapeDtypeStruct((total, 2 * half), ki...  10 us
    ppermute x4, waiting for transfers between devices, hop(): return lax.ppermute(value, 'ep', pairs)  9.58 us
    ppermute x4, starting transfers between devices, flip(): return lax.ppermute(value, 'ep', pairs)  9.03 us
    pallas_call x3, Pallas kernels, load(): pl.pallas_call(body, out_shape=pltpu.VMEM(value.shape, value.dtype), in_s...  6.13 us
  transfers between devices with their start and end apart: 40, of which 15 were waited for; matrix products, arithmetic and copies ran while one was open for 0% of the time, Pallas kernels for 18%

commit v1 on v0

--- a/solution.py
+++ b/solution.py
@@ -69,41 +69,33 @@
 def stage(tokens, routes, gate_levels):
     tok_rows, width = tokens.shape
     top = routes.shape[1]
-    direct = width % LANES == 0
+    assert tok_rows == LANES
+    tall = -(-width // LANES) * LANES
+    total = tall + 2 * top
 
     def body(routes_ref, levels_ref, tokens_ref, out_ref, held, small, sems):
-        target = out_ref.at[:, :width] if direct else held
         copies = [
+            pltpu.make_async_copy(tokens_ref, held, sems.at[2]),
             pltpu.make_async_copy(routes_ref, small.at[0], sems.at[0]),
             pltpu.make_async_copy(levels_ref, small.at[1], sems.at[1]),
-            pltpu.make_async_copy(tokens_ref, target, sems.at[2]),
         ]
         for copy in copies:
             copy.start()
-        lane = lax.broadcasted_iota(jnp.int32, (top, LANES), 1)
-        choice = lax.broadcasted_iota(jnp.int32, (top, LANES), 0)
-        marks = jnp.zeros((tok_rows, LANES), F32)
-        for i in range(2):
-            copies[i].wait()
-            spread = jnp.where(lane == choice + i * top, 1.0, 0.0).astype(BF16)
-            marks = marks + lax.dot_general(
-                small[i].astype(F32).astype(BF16),
-                spread,
-                (((0,), (0,)), ((), ())),
-                preferred_element_type=F32,
-            )
-        out_ref[:, width:] = marks.astype(BF16)
-        copies[2].wait()
-        if not direct:
-            out_ref[:, :width] = held[...]
-
-    return pl.pallas_call(
-        body,
-        out_shape=jax.ShapeDtypeStruct((tok_rows, width + LANES), BF16),
+        for copy in copies:
+            copy.wait()
+        for at in range(0, width, LANES):
+            wide = min(LANES, width - at)
+            out_ref[at : at + LANES, :wide] = held[:, at : at + wide]
+        marks = jnp.concatenate([small[0], small[1]], axis=0).astype(F32)
+        out_ref[tall:, :] = marks.astype(BF16)
+
+    return pl.pallas_call(
+        body,
+        out_shape=jax.ShapeDtypeStruct((total, LANES), BF16),
         in_specs=hbm(3),
         out_specs=vmem(1)[0],
         scratch_shapes=[
-            pltpu.VMEM((8, LANES) if direct else (tok_rows, width), BF16),
+            pltpu.VMEM((tok_rows, width), BF16),
             pltpu.VMEM((2, top, tok_rows), jnp.int32),
             pltpu.SemaphoreType.DMA((3,)),
         ],
@@ -113,7 +105,8 @@
 
 
 def pack(blocks, width, top, capacity, inner, outer):
-    tok_rows = blocks[0].shape[0]
+    tok_rows = LANES
+    tall = -(-width // LANES) * LANES
     span = -(-capacity // LANES) * LANES
     count = len(blocks)
 
@@ -125,7 +118,14 @@
         if count == 2:
             middle = (plane > 0) & (plane < outer - 1)
             block = jnp.where(middle, block, block_refs[1][...])
-        marks = block[:, width:].astype(F32)
+        choice = lax.broadcasted_iota(jnp.int32, (2 * top, LANES), 0)
+        spread = lax.broadcasted_iota(jnp.int32, (2 * top, LANES), 1) == choice
+        marks = lax.dot_general(
+            block[tall:],
+            jnp.where(spread, 1.0, 0.0).astype(BF16),
+            (((0,), (0,)), ((), ())),
+            preferred_element_type=F32,
+        )
         lane = lax.broadcasted_iota(jnp.int32, marks.shape, 1)
         levels = pltpu.roll(marks, marks.shape[1] - top, 1)
         inside = lane < top
@@ -143,15 +143,21 @@
         below = jnp.where(col < row, 1.0, 0.0).astype(BF16)
         slots = jnp.dot(below, gathered.astype(BF16), preferred_element_type=F32)
         place = lax.broadcasted_iota(jnp.int32, (tok_rows, span), 1).astype(F32)
-        data = block[:, :width]
+        data = jnp.concatenate(
+            [
+                block[at : at + LANES, : min(LANES, width - at)]
+                for at in range(0, width, LANES)
+            ],
+            axis=1,
+        )
         for j in range(inner):
             match = (place == slots[:, j : j + 1]) & (named[j] > 0.0)
             mix_ref[:, j * span : (j + 1) * span] = jnp.where(match, share[j], 0.0).astype(BF16)
             pick = jnp.where(match, 1.0, 0.0).astype(BF16)
             rows = lax.dot_general(
-                pick, data, (((0,), (0,)), ((), ())), preferred_element_type=F32
+                pick[:, :capacity], data, (((0,), (0,)), ((), ())), preferred_element_type=F32
             )
-            out_refs[j][...] = rows[:capacity].astype(BF16)
+            out_refs[j][...] = rows.astype(BF16)
 
     out = pl.pallas_call(
         body,
@@ -274,6 +280,31 @@
     )(mix, *rows, *partials)
 
 
+def close_sum(total, part):
+    tok_rows, width = total.shape
+    rows = tok_rows // PIECES
+
+    def body(total_ref, part_ref, out_ref, held, sems):
+        copies = []
+        for p in range(PIECES):
+            here = pl.ds(p * rows, rows)
+            held[here] = (total_ref[here] + part_ref[here].astype(F32)).astype(BF16)
+            copies.append(pltpu.make_async_copy(held.at[here], out_ref.at[here], sems.at[p]))
+            copies[-1].start()
+        for copy in copies:
+            copy.wait()
+
+    return pl.pallas_call(
+        body,
+        out_shape=jax.ShapeDtypeStruct((tok_rows, width), BF16),
+        in_specs=vmem(2),
+        out_specs=hbm(1)[0],
+        scratch_shapes=[pltpu.VMEM((tok_rows, width), BF16), pltpu.SemaphoreType.DMA((PIECES,))],
+        compiler_params=params(2),
+        name="close",
+    )(total, part)
+
+
 def on_device(tokens, routes, gate_levels, w_gate, w_up, w_down):
     ep_count, tp_count = lax.axis_size("ep"), lax.axis_size("tp")
     tok_rows, top_count = routes.shape
@@ -283,6 +314,7 @@
     width = tokens.shape[1]
     inner = inner_size(ep_count)
     outer = ep_count // inner
+    ordered = outer == 4 and tp_count == 2
 
     def hop(value, hops):
         pairs = [(a * inner + i, b * inner + i) for a, b in hops for i in range(inner)]
@@ -328,7 +360,7 @@
         return combine(returned, mix, partials, kind)
 
     own = stage(tokens, routes, gate_levels)
-    if outer != 4:
+    if not ordered:
         sent = [send([own])]
         sent += [send([flip(own, k)]) for k in range(1, outer)]
         partials = []
@@ -339,13 +371,14 @@
         mix, rows = sent[0]
         return gather(expert(rows, w_gate, w_up, w_down), mix, partials)
 
+    swap_middle, to_ends = [(1, 2), (2, 1)], [(1, 0), (2, 3)]
     beside = flip(own, 1)
-    across = hop(own, [(1, 2), (2, 1)])
+    across = hop(own, swap_middle)
     mix0, rows0 = send([own])
-    relayed = hop(beside, [(1, 2), (2, 1)])
-    outward = hop(across, [(1, 0), (2, 3)])
+    relayed = hop(beside, swap_middle)
+    outward = hop(across, to_ends)
     mix1, rows1 = send([beside])
-    last = hop(relayed, [(1, 0), (2, 3)])
+    last = hop(relayed, to_ends)
     mix2, rows2 = send([relayed, outward])
     mix3, rows3 = send([across, last])
     weights = [load(w_gate), load(w_up), load(w_down)]
@@ -353,7 +386,8 @@
     passed = flip(gather(made[2], mix2, []), 1)
     distant = flip(gather(made[3], mix3, [passed]), 3)
     close = flip(gather(made[1], mix1, []), 1)
-    return gather(made[0], mix0, [close, distant])
+    total = gather(made[0], mix0, [distant], F32)
+    return close_sum(total, close)
 
 
 def solution(mesh):

time: 152 us -> 160 us (1.053)
  the two profiles are of different devices: /device:TPU:14 before, /device:TPU:0 now
where the time goes in v1:
time: 160 us
  waiting for transfers between devices  90 us (56%)
  starting transfers between devices  38.7 us (24%)
  Pallas kernels  31 us (19%)
    ppermute x24, waiting for transfers between devices, near(): lax.ppermute(rows[j], 'ep', [(i, i ^ j) for i in range(ep_count)])  59.4 us
    ppermute x24, starting transfers between devices, near(): lax.ppermute(rows[j], 'ep', [(i, i ^ j) for i in range(ep_count)])  27.7 us
    ppermute x4, waiting for transfers between devices, flip(): return lax.ppermute(value, 'ep', pairs)  17.4 us
    ppermute x4, waiting for transfers between devices, hop(): return lax.ppermute(value, 'ep', pairs)  13.3 us
    pallas_call x8, Pallas kernels, lift(): pl.pallas_call(body, out_shape=jax.ShapeDtypeStruct((total, 2 * half), ki...  10 us
    ppermute x4, starting transfers between devices, flip(): return lax.ppermute(value, 'ep', pairs)  6.64 us
    pallas_call x3, Pallas kernels, load(): pl.pallas_call(body, out_shape=pltpu.VMEM(value.shape, value.dtype), in_s...  6.13 us
    pallas_call x4, Pallas kernels, lower(): pl.pallas_call(body, out_shape=[jax.ShapeDtypeStruct((capacity, width), B...  5.12 us
  transfers between devices with their start and end apart: 40, of which 19 were waited for; matrix products, arithmetic and copies ran while one was open for 0% of the time, Pallas kernels for 18%

profile of v1, /device:TPU:0, one launch (start us, length us, event | category | flops | bytes accessed | tf_op | source)
XLA Modules:
  0.0 160.3 jit_solution(1353128880079303697)
XLA Ops:
  0.0 1.1 stage.1.refs_0_
  1.1 3.1 %collective-permute-start.9 = (bf16[1808,128]{1,0:T(8,128)(2,1)S(1)}, bf16[1808,128]{1,0:T(8,128)(2,1)S(1)}, u32[]{:S(2)}, u32[]{:S(2)}) collective-permute-start(bf16[1808,128]{1,0:T(8,128)(2,1)S(1)} %stage.1.refs_0_), channel_id=1, source_target_pairs={{0,8},{2,10},{4,12},{6,14},{8,0},{10,2},{12,4},{14,6},{16,24},{18,... | collective-permute-start | bytes 1388552 | tf_op jit(solution)/shard_map/ppermute | solution.py:325
  4.3 0.7 collective-permute-start.8
  4.9 9.9 %collective-permute-done.9.refs_0_ = bf16[1808,128]{1,0:T(8,128)(2,1)S(1)} collective-permute-done((bf16[1808,128]{1,0:T(8,128)(2,1)S(1)}, bf16[1808,128]{1,0:T(8,128)(2,1)S(1)}, u32[]{:S(2)}, u32[]{:S(2)}) %collective-permute-start.9) | collective-permute-done | bytes 462880 | tf_op jit(solution)/shard_map/ppermute | solution.py:325
  14.9 0.7 collective-permute-start.10
  15.6 1.3 collective-permute-start.20
  16.9 1.3 collective-permute-start.11
  18.2 13.3 %collective-permute-done.20.refs_1_ = bf16[1808,128]{1,0:T(8,128)(2,1)S(1)} collective-permute-done((bf16[1808,128]{1,0:T(8,128)(2,1)S(1)}, bf16[1808,128]{1,0:T(8,128)(2,1)S(1)}, u32[]{:S(2)}, u32[]{:S(2)}) %collective-permute-start.20) | collective-permute-done | bytes 462880 | tf_op jit(solution)/shard_map/ppermute | solution.py:321
  31.5 1.1 pack.6
  32.6 1.6 collective-permute-start.21
  34.1 1.5 collective-permute-start.22
  36.1 2.0 %load.3.refs_4_ = bf16[1792,1024]{1,0:T(8,128)(2,1)S(1)} custom-call(bf16[1792,1024]{1,0:T(8,128)(2,1)} %bitcast.5), custom_call_target="tpu_custom_call" | custom-call | tf_op jit(solution)/shard_map/load/pallas_call | solution.py:58
  38.2 2.0 %load.4.refs_5_ = bf16[1792,1024]{1,0:T(8,128)(2,1)S(1)} custom-call(bf16[1792,1024]{1,0:T(8,128)(2,1)} %bitcast.6), custom_call_target="tpu_custom_call" | custom-call | tf_op jit(solution)/shard_map/load/pallas_call | solution.py:58
  40.2 0.8 collective-permute-done.21.refs_1_
  41.0 4.0 %collective-permute-done.22.refs_2_ = bf16[72,1792]{1,0:T(8,128)(2,1)S(1)} collective-permute-done((bf16[72,1792]{1,0:T(8,128)(2,1)S(1)}, bf16[72,1792]{1,0:T(8,128)(2,1)S(1)}, u32[]{:S(2)}, u32[]{:S(2)}) %collective-permute-start.22) | collective-permute-done | bytes 258080 | tf_op jit(solution)/shard_map/ppermute | solution.py:330
  45.0 1.3 lift.13
  46.4 1.1 pack.5
  47.5 1.3 collective-permute-start.12
  48.8 0.8 collective-permute-start.13
  49.6 1.4 collective-permute-start.14
  51.0 5.6 %collective-permute-done.12.refs_1_ = bf16[72,1792]{1,0:T(8,128)(2,1)S(1)} collective-permute-done((bf16[72,1792]{1,0:T(8,128)(2,1)S(1)}, bf16[72,1792]{1,0:T(8,128)(2,1)S(1)}, u32[]{:S(2)}, u32[]{:S(2)}) %collective-permute-start.12) | collective-permute-done | bytes 258080 | tf_op jit(solution)/shard_map/ppermute | solution.py:330
  56.6 4.4 %collective-permute-done.13.refs_2_ = bf16[72,1792]{1,0:T(8,128)(2,1)S(1)} collective-permute-done((bf16[72,1792]{1,0:T(8,128)(2,1)S(1)}, bf16[72,1792]{1,0:T(8,128)(2,1)S(1)}, u32[]{:S(2)}, u32[]{:S(2)}) %collective-permute-start.13) | collective-permute-done | bytes 258080 | tf_op jit(solution)/shard_map/ppermute | solution.py:330
  61.0 1.6 %collective-permute-done.14.refs_3_ = bf16[72,1792]{1,0:T(8,128)(2,1)S(1)} collective-permute-done((bf16[72,1792]{1,0:T(8,128)(2,1)S(1)}, bf16[72,1792]{1,0:T(8,128)(2,1)S(1)}, u32[]{:S(2)}, u32[]{:S(2)}) %collective-permute-start.14) | collective-permute-done | bytes 258080 | tf_op jit(solution)/shard_map/ppermute | solution.py:330
  62.6 1.3 lift.11
  64.0 1.1 pack.7
  65.1 0.8 collective-permute-start.31
  65.9 1.5 collective-permute-start.32
  67.4 1.2 collective-permute-start.33
  68.6 1.2 lift.12.keep_ref
  70.2 1.1 pack.4
  71.3 2.9 %collective-permute-done.31.refs_1_ = bf16[72,1792]{1,0:T(8,128)(2,1)S(1)} collective-permute-done((bf16[72,1792]{1,0:T(8,128)(2,1)S(1)}, bf16[72,1792]{1,0:T(8,128)(2,1)S(1)}, u32[]{:S(2)}, u32[]{:S(2)}) %collective-permute-start.31) | collective-permute-done | bytes 258080 | tf_op jit(solution)/shard_map/ppermute | solution.py:330
  74.2 0.8 collective-permute-start
  75.0 4.8 %collective-permute-done.32.refs_2_ = bf16[72,1792]{1,0:T(8,128)(2,1)S(1)} collective-permute-done((bf16[72,1792]{1,0:T(8,128)(2,1)S(1)}, bf16[72,1792]{1,0:T(8,128)(2,1)S(1)}, u32[]{:S(2)}, u32[]{:S(2)}) %collective-permute-start.32) | collective-permute-done | bytes 258080 | tf_op jit(solution)/shard_map/ppermute | solution.py:330
  79.8 1.9 %collective-permute-start.1 = (bf16[72,1792]{1,0:T(8,128)(2,1)S(1)}, bf16[72,1792]{1,0:T(8,128)(2,1)S(1)}, u32[]{:S(2)}, u32[]{:S(2)}) collective-permute-start(bf16[72,1792]{1,0:T(8,128)(2,1)S(1)} %get-tuple-element.44), channel_id=1, source_target_pairs={{0,4},{2,6},{4,0},{6,2},{8,12},{10,14},{12,8},{14,10},{16,20},{18,... | collective-permute-start | bytes 774152 | tf_op jit(solution)/shard_map/ppermute | solution.py:330
  81.8 1.3 lift.15
  83.1 2.0 %load.5.w_ref = bf16[1024,1792]{1,0:T(8,128)(2,1)S(1)} custom-call(bf16[1024,1792]{1,0:T(8,128)(2,1)} %bitcast.7), custom_call_target="tpu_custom_call" | custom-call | tf_op jit(solution)/shard_map/load/pallas_call | solution.py:58
  85.3 1.2 lower.6
  86.5 1.6 collective-permute-start.26
  88.1 1.9 %collective-permute-start.27 = (bf16[72,1792]{1,0:T(8,128)(2,1)S(1)}, bf16[72,1792]{1,0:T(8,128)(2,1)S(1)}, u32[]{:S(2)}, u32[]{:S(2)}) collective-permute-start(bf16[72,1792]{1,0:T(8,128)(2,1)S(1)} %get-tuple-element.66), channel_id=1, source_target_pairs={{0,4},{2,6},{4,0},{6,2},{8,12},{10,14},{12,8},{14,10},{16,20},{18,... | collective-permute-start | bytes 774152 | tf_op jit(solution)/shard_map/ppermute | solution.py:330
  90.1 1.2 lift.10.keep_ref
  91.6 3.7 %collective-permute-done.2.refs_3_ = bf16[72,1792]{1,0:T(8,128)(2,1)S(1)} collective-permute-done((bf16[72,1792]{1,0:T(8,128)(2,1)S(1)}, bf16[72,1792]{1,0:T(8,128)(2,1)S(1)}, u32[]{:S(2)}, u32[]{:S(2)}) %collective-permute-start.2) | collective-permute-done | bytes 258080 | tf_op jit(solution)/shard_map/ppermute | solution.py:330
  95.3 1.3 lift.9
  96.6 2.9 %collective-permute-done.26.refs_1_ = bf16[72,1792]{1,0:T(8,128)(2,1)S(1)} collective-permute-done((bf16[72,1792]{1,0:T(8,128)(2,1)S(1)}, bf16[72,1792]{1,0:T(8,128)(2,1)S(1)}, u32[]{:S(2)}, u32[]{:S(2)}) %collective-permute-start.26) | collective-permute-done | bytes 258080 | tf_op jit(solution)/shard_map/ppermute | solution.py:330
  99.4 1.3 collective-permute-done.27.refs_2_
  100.7 5.1 %collective-permute-done.28.refs_3_ = bf16[72,1792]{1,0:T(8,128)(2,1)S(1)} collective-permute-done((bf16[72,1792]{1,0:T(8,128)(2,1)S(1)}, bf16[72,1792]{1,0:T(8,128)(2,1)S(1)}, u32[]{:S(2)}, u32[]{:S(2)}) %collective-permute-start.28) | collective-permute-done | bytes 258080 | tf_op jit(solution)/shard_map/ppermute | solution.py:330
  107.0 1.2 lift.14.keep_ref
  108.6 1.4 lower.5
  110.9 1.2 lower.7
  112.2 1.3 collective-permute-start.36
  113.5 1.9 %collective-permute-start.37 = (bf16[72,1792]{1,0:T(8,128)(2,1)S(1)}, bf16[72,1792]{1,0:T(8,128)(2,1)S(1)}, u32[]{:S(2)}, u32[]{:S(2)}) collective-permute-start(bf16[72,1792]{1,0:T(8,128)(2,1)S(1)} %get-tuple-element.75), channel_id=1, source_target_pairs={{0,4},{2,6},{4,0},{6,2},{8,12},{10,14},{12,8},{14,10},{16,20},{18,... | collective-permute-start | bytes 774152 | tf_op jit(solution)/shard_map/ppermute | solution.py:330
  115.4 3.2 %collective-permute-done.29.refs_4_ = bf16[128,1792]{1,0:T(8,128)(2,1)S(1)} collective-permute-done((bf16[128,1792]{1,0:T(8,128)(2,1)S(1)}, bf16[128,1792]{1,0:T(8,128)(2,1)S(1)}, u32[]{:S(2)}, u32[]{:S(2)}) %collective-permute-start.29) | collective-permute-done | bytes 458784 | tf_op jit(solution)/shard_map/ppermute | solution.py:325
  119.2 2.4 %collective-permute-start.19 = (bf16[72,1792]{1,0:T(8,128)(2,1)S(1)}, bf16[72,1792]{1,0:T(8,128)(2,1)S(1)}, u32[]{:S(2)}, u32[]{:S(2)}) collective-permute-start(bf16[72,1792]{1,0:T(8,128)(2,1)S(1)} %get-tuple-element.58), channel_id=1, source_target_pairs={{0,6},{2,4},{4,2},{6,0},{8,14},{10,12},{12,10},{14,8},{16,22},{18,... | collective-permute-start | bytes 774152 | tf_op jit(solution)/shard_map/ppermute | solution.py:330
  121.6 1.3 lift.8.keep_ref
  123.2 11.7 %collective-permute-done.19.refs_3_ = bf16[72,1792]{1,0:T(8,128)(2,1)S(1)} collective-permute-done((bf16[72,1792]{1,0:T(8,128)(2,1)S(1)}, bf16[72,1792]{1,0:T(8,128)(2,1)S(1)}, u32[]{:S(2)}, u32[]{:S(2)}) %collective-permute-start.19) | collective-permute-done | bytes 258080 | tf_op jit(solution)/shard_map/ppermute | solution.py:330
  135.5 2.7 %collective-permute-start.30 = (bf16[128,1792]{1,0:T(8,128)(2,1)S(1)}, bf16[128,1792]{1,0:T(8,128)(2,1)S(1)}, u32[]{:S(2)}, u32[]{:S(2)}) collective-permute-start(bf16[128,1792]{1,0:T(8,128)(2,1)S(1)} %combine.5), channel_id=1, source_target_pairs={{0,24},{2,26},{4,28},{6,30},{8,16},{10,18},{12,20},{14,22},{16,8},... | collective-permute-start | bytes 1376264 | tf_op jit(solution)/shard_map/ppermute | solution.py:325
  139.2 1.2 lower.4
  140.4 0.8 collective-permute-start.5
  141.2 1.5 collective-permute-start.6
  142.6 1.3 collective-permute-start.7
  144.0 5.6 %collective-permute-done.5.refs_1_ = bf16[72,1792]{1,0:T(8,128)(2,1)S(1)} collective-permute-done((bf16[72,1792]{1,0:T(8,128)(2,1)S(1)}, bf16[72,1792]{1,0:T(8,128)(2,1)S(1)}, u32[]{:S(2)}, u32[]{:S(2)}) %collective-permute-start.5) | collective-permute-done | bytes 258080 | tf_op jit(solution)/shard_map/ppermute | solution.py:330
  149.6 3.0 %collective-permute-done.6.refs_2_ = bf16[72,1792]{1,0:T(8,128)(2,1)S(1)} collective-permute-done((bf16[72,1792]{1,0:T(8,128)(2,1)S(1)}, bf16[72,1792]{1,0:T(8,128)(2,1)S(1)}, u32[]{:S(2)}, u32[]{:S(2)}) %collective-permute-start.6) | collective-permute-done | bytes 258080 | tf_op jit(solution)/shard_map/ppermute | solution.py:330
  152.6 1.8 %collective-permute-done.7.refs_3_ = bf16[72,1792]{1,0:T(8,128)(2,1)S(1)} collective-permute-done((bf16[72,1792]{1,0:T(8,128)(2,1)S(1)}, bf16[72,1792]{1,0:T(8,128)(2,1)S(1)}, u32[]{:S(2)}, u32[]{:S(2)}) %collective-permute-start.7) | collective-permute-done | bytes 258080 | tf_op jit(solution)/shard_map/ppermute | solution.py:330
  155.0 4.2 %collective-permute-done.39.part_ref = bf16[128,1792]{1,0:T(8,128)(2,1)S(1)} collective-permute-done((bf16[128,1792]{1,0:T(8,128)(2,1)S(1)}, bf16[128,1792]{1,0:T(8,128)(2,1)S(1)}, u32[]{:S(2)}, u32[]{:S(2)}) %collective-permute-start.39) | collective-permute-done | bytes 458784 | tf_op jit(solution)/shard_map/ppermute | solution.py:325
  159.3 0.8 close.1
  (45 shorter events, 6.8 us)
Async XLA Ops:
  1.1 13.7 %collective-permute-start.9 = (bf16[1808,128]{1,0:T(8,128)(2,1)S(1)}, bf16[1808,128]{1,0:T(8,128)(2,1)S(1)}, u32[]{:S(2)}, u32[]{:S(2)}) collective-permute-start(bf16[1808,128]{1,0:T(8,128)(2,1)S(1)} %stage.1.refs_0_), channel_id=1, source_target_pairs={{0,8},{2,10},{4,12},{6,14},{8,0},{10,2},{12,4},{14,6},{16,24},{18,... | collective-permute-start | bytes 1388552 | tf_op jit(solution)/shard_map/ppermute | solution.py:325
  4.3 11.3 %collective-permute-start.8 = (bf16[1808,128]{1,0:T(8,128)(2,1)S(1)}, bf16[1808,128]{1,0:T(8,128)(2,1)S(1)}, u32[]{:S(2)}, u32[]{:S(2)}) collective-permute-start(bf16[1808,128]{1,0:T(8,128)(2,1)S(1)} %stage.1.refs_0_), channel_id=1, source_target_pairs={{8,16},{10,18},{12,20},{14,22},{16,8},{18,10},{20,12},{22,14},{9,1... | collective-permute-start | bytes 1388552 | tf_op jit(solution)/shard_map/ppermute | solution.py:321
  14.9 2.0 %collective-permute-start.10 = (bf16[1808,128]{1,0:T(8,128)(2,1)S(1)}, bf16[1808,128]{1,0:T(8,128)(2,1)S(1)}, u32[]{:S(2)}, u32[]{:S(2)}) collective-permute-start(bf16[1808,128]{1,0:T(8,128)(2,1)S(1)} %collective-permute-done.9.refs_0_), channel_id=1, source_target_pairs={{8,16},{10,18},{12,20},{14,22},{16,8},{18,10},{20,12},{22,14},{9,1... | collective-permute-start | bytes 1388552 | tf_op jit(solution)/shard_map/ppermute | solution.py:321
  15.6 15.9 %collective-permute-start.20 = (bf16[1808,128]{1,0:T(8,128)(2,1)S(1)}, bf16[1808,128]{1,0:T(8,128)(2,1)S(1)}, u32[]{:S(2)}, u32[]{:S(2)}) collective-permute-start(bf16[1808,128]{1,0:T(8,128)(2,1)S(1)} %collective-permute-done.8.refs_0_), channel_id=1, source_target_pairs={{8,0},{10,2},{12,4},{14,6},{16,24},{18,26},{20,28},{22,30},{9,1},{... | collective-permute-start | bytes 1388552 | tf_op jit(solution)/shard_map/ppermute | solution.py:321
  16.9 29.5 %collective-permute-start.11 = (bf16[1808,128]{1,0:T(8,128)(2,1)S(1)}, bf16[1808,128]{1,0:T(8,128)(2,1)S(1)}, u32[]{:S(2)}, u32[]{:S(2)}) collective-permute-start(bf16[1808,128]{1,0:T(8,128)(2,1)S(1)} %collective-permute-done.10.refs_0_), channel_id=1, source_target_pairs={{8,0},{10,2},{12,4},{14,6},{16,24},{18,26},{20,28},{22,30},{9,1},{... | collective-permute-start | bytes 1388552 | tf_op jit(solution)/shard_map/ppermute | solution.py:321
  32.6 8.5 %collective-permute-start.21 = (bf16[72,1792]{1,0:T(8,128)(2,1)S(1)}, bf16[72,1792]{1,0:T(8,128)(2,1)S(1)}, u32[]{:S(2)}, u32[]{:S(2)}) collective-permute-start(bf16[72,1792]{1,0:T(8,128)(2,1)S(1)} %get-tuple-element.61), channel_id=1, source_target_pairs={{0,2},{2,0},{4,6},{6,4},{8,10},{10,8},{12,14},{14,12},{16,18},{18,... | collective-permute-start | bytes 774152 | tf_op jit(solution)/shard_map/ppermute | solution.py:330
  34.1 10.9 %collective-permute-start.22 = (bf16[72,1792]{1,0:T(8,128)(2,1)S(1)}, bf16[72,1792]{1,0:T(8,128)(2,1)S(1)}, u32[]{:S(2)}, u32[]{:S(2)}) collective-permute-start(bf16[72,1792]{1,0:T(8,128)(2,1)S(1)} %get-tuple-element.62), channel_id=1, source_target_pairs={{0,4},{2,6},{4,0},{6,2},{8,12},{10,14},{12,8},{14,10},{16,20},{18,... | collective-permute-start | bytes 774152 | tf_op jit(solution)/shard_map/ppermute | solution.py:330
  35.6 9.4 %collective-permute-start.23 = (bf16[72,1792]{1,0:T(8,128)(2,1)S(1)}, bf16[72,1792]{1,0:T(8,128)(2,1)S(1)}, u32[]{:S(2)}, u32[]{:S(2)}) collective-permute-start(bf16[72,1792]{1,0:T(8,128)(2,1)S(1)} %get-tuple-element.63), channel_id=1, source_target_pairs={{0,6},{2,4},{4,2},{6,0},{8,14},{10,12},{12,10},{14,8},{16,22},{18,... | collective-permute-start | bytes 774152 | tf_op jit(solution)/shard_map/ppermute | solution.py:330
  46.3 23.6 %collective-permute-start.24 = (bf16[288,1024]{1,0:T(8,128)(2,1)S(1)}, bf16[288,1024]{1,0:T(8,128)(2,1)S(1)}, u32[]{:S(2)}, u32[]{:S(2)}) collective-permute-start(bf16[288,1024]{1,0:T(8,128)(2,1)S(1)} %lift.13), channel_id=1, source_target_pairs={{0,1},{1,0},{2,3},{3,2},{4,5},{5,4},{6,7},{7,6},{8,9},{9,8},{10,11... | collective-permute-start | bytes 1769480 | tf_op jit(solution)/shard_map/ppermute | solution.py:334
  47.5 9.2 %collective-permute-start.12 = (bf16[72,1792]{1,0:T(8,128)(2,1)S(1)}, bf16[72,1792]{1,0:T(8,128)(2,1)S(1)}, u32[]{:S(2)}, u32[]{:S(2)}) collective-permute-start(bf16[72,1792]{1,0:T(8,128)(2,1)S(1)} %get-tuple-element.52), channel_id=1, source_target_pairs={{0,2},{2,0},{4,6},{6,4},{8,10},{10,8},{12,14},{14,12},{16,18},{18,... | collective-permute-start | bytes 774152 | tf_op jit(solution)/shard_map/ppermute | solution.py:330
  48.8 12.2 %collective-permute-start.13 = (bf16[72,1792]{1,0:T(8,128)(2,1)S(1)}, bf16[72,1792]{1,0:T(8,128)(2,1)S(1)}, u32[]{:S(2)}, u32[]{:S(2)}) collective-permute-start(bf16[72,1792]{1,0:T(8,128)(2,1)S(1)} %get-tuple-element.53), channel_id=1, source_target_pairs={{0,4},{2,6},{4,0},{6,2},{8,12},{10,14},{12,8},{14,10},{16,20},{18,... | collective-permute-start | bytes 774152 | tf_op jit(solution)/shard_map/ppermute | solution.py:330
  49.6 13.0 %collective-permute-start.14 = (bf16[72,1792]{1,0:T(8,128)(2,1)S(1)}, bf16[72,1792]{1,0:T(8,128)(2,1)S(1)}, u32[]{:S(2)}, u32[]{:S(2)}) collective-permute-start(bf16[72,1792]{1,0:T(8,128)(2,1)S(1)} %get-tuple-element.54), channel_id=1, source_target_pairs={{0,6},{2,4},{4,2},{6,0},{8,14},{10,12},{12,10},{14,8},{16,22},{18,... | collective-permute-start | bytes 774152 | tf_op jit(solution)/shard_map/ppermute | solution.py:330
  63.9 26.1 %collective-permute-start.15 = (bf16[288,1024]{1,0:T(8,128)(2,1)S(1)}, bf16[288,1024]{1,0:T(8,128)(2,1)S(1)}, u32[]{:S(2)}, u32[]{:S(2)}) collective-permute-start(bf16[288,1024]{1,0:T(8,128)(2,1)S(1)} %lift.11), channel_id=1, source_target_pairs={{0,1},{1,0},{2,3},{3,2},{4,5},{5,4},{6,7},{7,6},{8,9},{9,8},{10,11... | collective-permute-start | bytes 1769480 | tf_op jit(solution)/shard_map/ppermute | solution.py:334
  65.1 9.2 %collective-permute-start.31 = (bf16[72,1792]{1,0:T(8,128)(2,1)S(1)}, bf16[72,1792]{1,0:T(8,128)(2,1)S(1)}, u32[]{:S(2)}, u32[]{:S(2)}) collective-permute-start(bf16[72,1792]{1,0:T(8,128)(2,1)S(1)} %get-tuple-element.70), channel_id=1, source_target_pairs={{0,2},{2,0},{4,6},{6,4},{8,10},{10,8},{12,14},{14,12},{16,18},{18,... | collective-permute-start | bytes 774152 | tf_op jit(solution)/shard_map/ppermute | solution.py:330
  65.9 13.9 %collective-permute-start.32 = (bf16[72,1792]{1,0:T(8,128)(2,1)S(1)}, bf16[72,1792]{1,0:T(8,128)(2,1)S(1)}, u32[]{:S(2)}, u32[]{:S(2)}) collective-permute-start(bf16[72,1792]{1,0:T(8,128)(2,1)S(1)} %get-tuple-element.71), channel_id=1, source_target_pairs={{0,4},{2,6},{4,0},{6,2},{8,12},{10,14},{12,8},{14,10},{16,20},{18,... | collective-permute-start | bytes 774152 | tf_op jit(solution)/shard_map/ppermute | solution.py:330
  67.4 14.3 %collective-permute-start.33 = (bf16[72,1792]{1,0:T(8,128)(2,1)S(1)}, bf16[72,1792]{1,0:T(8,128)(2,1)S(1)}, u32[]{:S(2)}, u32[]{:S(2)}) collective-permute-start(bf16[72,1792]{1,0:T(8,128)(2,1)S(1)} %get-tuple-element.72), channel_id=1, source_target_pairs={{0,6},{2,4},{4,2},{6,0},{8,14},{10,12},{12,10},{14,8},{16,22},{18,... | collective-permute-start | bytes 774152 | tf_op jit(solution)/shard_map/ppermute | solution.py:330
  70.1 15.1 %collective-permute-start.25 = (bf16[288,512]{1,0:T(8,128)(2,1)S(1)}, bf16[288,512]{1,0:T(8,128)(2,1)S(1)}, u32[]{:S(2)}, u32[]{:S(2)}) collective-permute-start(bf16[288,512]{1,0:T(8,128)(2,1)S(1)} %activate.6.own_ref), channel_id=1, source_target_pairs={{0,1},{1,0},{2,3},{3,2},{4,5},{5,4},{6,7},{7,6},{8,9},{9,8},{10,11... | collective-permute-start | bytes 884744 | tf_op jit(solution)/shard_map/ppermute | solution.py:334
  74.2 12.3 %collective-permute-start = (bf16[72,1792]{1,0:T(8,128)(2,1)S(1)}, bf16[72,1792]{1,0:T(8,128)(2,1)S(1)}, u32[]{:S(2)}, u32[]{:S(2)}) collective-permute-start(bf16[72,1792]{1,0:T(8,128)(2,1)S(1)} %get-tuple-element.43), channel_id=1, source_target_pairs={{0,2},{2,0},{4,6},{6,4},{8,10},{10,8},{12,14},{14,12},{16,18},{18,... | collective-permute-start | bytes 774152 | tf_op jit(solution)/shard_map/ppermute | solution.py:330
  79.8 8.3 %collective-permute-start.1 = (bf16[72,1792]{1,0:T(8,128)(2,1)S(1)}, bf16[72,1792]{1,0:T(8,128)(2,1)S(1)}, u32[]{:S(2)}, u32[]{:S(2)}) collective-permute-start(bf16[72,1792]{1,0:T(8,128)(2,1)S(1)} %get-tuple-element.44), channel_id=1, source_target_pairs={{0,4},{2,6},{4,0},{6,2},{8,12},{10,14},{12,8},{14,10},{16,20},{18,... | collective-permute-start | bytes 774152 | tf_op jit(solution)/shard_map/ppermute | solution.py:330
  83.1 25.2 %collective-permute-start.34 = (bf16[288,1024]{1,0:T(8,128)(2,1)S(1)}, bf16[288,1024]{1,0:T(8,128)(2,1)S(1)}, u32[]{:S(2)}, u32[]{:S(2)}) collective-permute-start(bf16[288,1024]{1,0:T(8,128)(2,1)S(1)} %lift.15), channel_id=1, source_target_pairs={{0,1},{1,0},{2,3},{3,2},{4,5},{5,4},{6,7},{7,6},{8,9},{9,8},{10,11... | collective-permute-start | bytes 1769480 | tf_op jit(solution)/shard_map/ppermute | solution.py:334
  85.2 10.1 %collective-permute-start.2 = (bf16[72,1792]{1,0:T(8,128)(2,1)S(1)}, bf16[72,1792]{1,0:T(8,128)(2,1)S(1)}, u32[]{:S(2)}, u32[]{:S(2)}) collective-permute-start(bf16[72,1792]{1,0:T(8,128)(2,1)S(1)} %get-tuple-element.45), channel_id=1, source_target_pairs={{0,6},{2,4},{4,2},{6,0},{8,14},{10,12},{12,10},{14,8},{16,22},{18,... | collective-permute-start | bytes 774152 | tf_op jit(solution)/shard_map/ppermute | solution.py:330
  86.5 12.9 %collective-permute-start.26 = (bf16[72,1792]{1,0:T(8,128)(2,1)S(1)}, bf16[72,1792]{1,0:T(8,128)(2,1)S(1)}, u32[]{:S(2)}, u32[]{:S(2)}) collective-permute-start(bf16[72,1792]{1,0:T(8,128)(2,1)S(1)} %get-tuple-element.65), channel_id=1, source_target_pairs={{0,2},{2,0},{4,6},{6,4},{8,10},{10,8},{12,14},{14,12},{16,18},{18,... | collective-permute-start | bytes 774152 | tf_op jit(solution)/shard_map/ppermute | solution.py:330
  88.1 12.6 %collective-permute-start.27 = (bf16[72,1792]{1,0:T(8,128)(2,1)S(1)}, bf16[72,1792]{1,0:T(8,128)(2,1)S(1)}, u32[]{:S(2)}, u32[]{:S(2)}) collective-permute-start(bf16[72,1792]{1,0:T(8,128)(2,1)S(1)} %get-tuple-element.66), channel_id=1, source_target_pairs={{0,4},{2,6},{4,0},{6,2},{8,12},{10,14},{12,8},{14,10},{16,20},{18,... | collective-permute-start | bytes 774152 | tf_op jit(solution)/shard_map/ppermute | solution.py:330
  90.1 15.8 %collective-permute-start.28 = (bf16[72,1792]{1,0:T(8,128)(2,1)S(1)}, bf16[72,1792]{1,0:T(8,128)(2,1)S(1)}, u32[]{:S(2)}, u32[]{:S(2)}) collective-permute-start(bf16[72,1792]{1,0:T(8,128)(2,1)S(1)} %get-tuple-element.67), channel_id=1, source_target_pairs={{0,6},{2,4},{4,2},{6,0},{8,14},{10,12},{12,10},{14,8},{16,22},{18,... | collective-permute-start | bytes 774152 | tf_op jit(solution)/shard_map/ppermute | solution.py:330
  95.3 13.3 %collective-permute-start.16 = (bf16[288,512]{1,0:T(8,128)(2,1)S(1)}, bf16[288,512]{1,0:T(8,128)(2,1)S(1)}, u32[]{:S(2)}, u32[]{:S(2)}) collective-permute-start(bf16[288,512]{1,0:T(8,128)(2,1)S(1)} %activate.5.own_ref), channel_id=1, source_target_pairs={{0,1},{1,0},{2,3},{3,2},{4,5},{5,4},{6,7},{7,6},{8,9},{9,8},{10,11... | collective-permute-start | bytes 884744 | tf_op jit(solution)/shard_map/ppermute | solution.py:334
  99.4 14.0 %collective-permute-start.3 = (bf16[288,1024]{1,0:T(8,128)(2,1)S(1)}, bf16[288,1024]{1,0:T(8,128)(2,1)S(1)}, u32[]{:S(2)}, u32[]{:S(2)}) collective-permute-start(bf16[288,1024]{1,0:T(8,128)(2,1)S(1)} %lift.9), channel_id=1, source_target_pairs={{0,1},{1,0},{2,3},{3,2},{4,5},{5,4},{6,7},{7,6},{8,9},{9,8},{10,11... | collective-permute-start | bytes 1769480 | tf_op jit(solution)/shard_map/ppermute | solution.py:334
  106.5 12.1 %collective-permute-start.29 = (bf16[128,1792]{1,0:T(8,128)(2,1)S(1)}, bf16[128,1792]{1,0:T(8,128)(2,1)S(1)}, u32[]{:S(2)}, u32[]{:S(2)}) collective-permute-start(bf16[128,1792]{1,0:T(8,128)(2,1)S(1)} %combine.4), channel_id=1, source_target_pairs={{0,8},{2,10},{4,12},{6,14},{8,0},{10,2},{12,4},{14,6},{16,24},{18,... | collective-permute-start | bytes 1376264 | tf_op jit(solution)/shard_map/ppermute | solution.py:325
  108.5 2.4 %collective-permute-start.35 = (bf16[288,512]{1,0:T(8,128)(2,1)S(1)}, bf16[288,512]{1,0:T(8,128)(2,1)S(1)}, u32[]{:S(2)}, u32[]{:S(2)}) collective-permute-start(bf16[288,512]{1,0:T(8,128)(2,1)S(1)} %activate.7.own_ref), channel_id=1, source_target_pairs={{0,1},{1,0},{2,3},{3,2},{4,5},{5,4},{6,7},{7,6},{8,9},{9,8},{10,11... | collective-permute-start | bytes 884744 | tf_op jit(solution)/shard_map/ppermute | solution.py:334
  110.0 9.2 %collective-permute-start.17 = (bf16[72,1792]{1,0:T(8,128)(2,1)S(1)}, bf16[72,1792]{1,0:T(8,128)(2,1)S(1)}, u32[]{:S(2)}, u32[]{:S(2)}) collective-permute-start(bf16[72,1792]{1,0:T(8,128)(2,1)S(1)} %get-tuple-element.56), channel_id=1, source_target_pairs={{0,2},{2,0},{4,6},{6,4},{8,10},{10,8},{12,14},{14,12},{16,18},{18,... | collective-permute-start | bytes 774152 | tf_op jit(solution)/shard_map/ppermute | solution.py:330
  110.4 12.6 %collective-permute-start.18 = (bf16[72,1792]{1,0:T(8,128)(2,1)S(1)}, bf16[72,1792]{1,0:T(8,128)(2,1)S(1)}, u32[]{:S(2)}, u32[]{:S(2)}) collective-permute-start(bf16[72,1792]{1,0:T(8,128)(2,1)S(1)} %get-tuple-element.57), channel_id=1, source_target_pairs={{0,4},{2,6},{4,0},{6,2},{8,12},{10,14},{12,8},{14,10},{16,20},{18,... | collective-permute-start | bytes 774152 | tf_op jit(solution)/shard_map/ppermute | solution.py:330
  112.2 26.0 %collective-permute-start.36 = (bf16[72,1792]{1,0:T(8,128)(2,1)S(1)}, bf16[72,1792]{1,0:T(8,128)(2,1)S(1)}, u32[]{:S(2)}, u32[]{:S(2)}) collective-permute-start(bf16[72,1792]{1,0:T(8,128)(2,1)S(1)} %get-tuple-element.74), channel_id=1, source_target_pairs={{0,2},{2,0},{4,6},{6,4},{8,10},{10,8},{12,14},{14,12},{16,18},{18,... | collective-permute-start | bytes 774152 | tf_op jit(solution)/shard_map/ppermute | solution.py:330
  113.5 24.7 %collective-permute-start.37 = (bf16[72,1792]{1,0:T(8,128)(2,1)S(1)}, bf16[72,1792]{1,0:T(8,128)(2,1)S(1)}, u32[]{:S(2)}, u32[]{:S(2)}) collective-permute-start(bf16[72,1792]{1,0:T(8,128)(2,1)S(1)} %get-tuple-element.75), channel_id=1, source_target_pairs={{0,4},{2,6},{4,0},{6,2},{8,12},{10,14},{12,8},{14,10},{16,20},{18,... | collective-permute-start | bytes 774152 | tf_op jit(solution)/shard_map/ppermute | solution.py:330
  118.6 19.5 %collective-permute-start.38 = (bf16[72,1792]{1,0:T(8,128)(2,1)S(1)}, bf16[72,1792]{1,0:T(8,128)(2,1)S(1)}, u32[]{:S(2)}, u32[]{:S(2)}) collective-permute-start(bf16[72,1792]{1,0:T(8,128)(2,1)S(1)} %get-tuple-element.76), channel_id=1, source_target_pairs={{0,6},{2,4},{4,2},{6,0},{8,14},{10,12},{12,10},{14,8},{16,22},{18,... | collective-permute-start | bytes 774152 | tf_op jit(solution)/shard_map/ppermute | solution.py:330
  119.2 15.7 %collective-permute-start.19 = (bf16[72,1792]{1,0:T(8,128)(2,1)S(1)}, bf16[72,1792]{1,0:T(8,128)(2,1)S(1)}, u32[]{:S(2)}, u32[]{:S(2)}) collective-permute-start(bf16[72,1792]{1,0:T(8,128)(2,1)S(1)} %get-tuple-element.58), channel_id=1, source_target_pairs={{0,6},{2,4},{4,2},{6,0},{8,14},{10,12},{12,10},{14,8},{16,22},{18,... | collective-permute-start | bytes 774152 | tf_op jit(solution)/shard_map/ppermute | solution.py:330
  123.1 16.1 %collective-permute-start.4 = (bf16[288,512]{1,0:T(8,128)(2,1)S(1)}, bf16[288,512]{1,0:T(8,128)(2,1)S(1)}, u32[]{:S(2)}, u32[]{:S(2)}) collective-permute-start(bf16[288,512]{1,0:T(8,128)(2,1)S(1)} %activate.4.own_ref), channel_id=1, source_target_pairs={{0,1},{1,0},{2,3},{3,2},{4,5},{5,4},{6,7},{7,6},{8,9},{9,8},{10,11... | collective-permute-start | bytes 884744 | tf_op jit(solution)/shard_map/ppermute | solution.py:334
  135.5 18.9 %collective-permute-start.30 = (bf16[128,1792]{1,0:T(8,128)(2,1)S(1)}, bf16[128,1792]{1,0:T(8,128)(2,1)S(1)}, u32[]{:S(2)}, u32[]{:S(2)}) collective-permute-start(bf16[128,1792]{1,0:T(8,128)(2,1)S(1)} %combine.5), channel_id=1, source_target_pairs={{0,24},{2,26},{4,28},{6,30},{8,16},{10,18},{12,20},{14,22},{16,8},... | collective-permute-start | bytes 1376264 | tf_op jit(solution)/shard_map/ppermute | solution.py:325
  138.8 20.5 %collective-permute-start.39 = (bf16[128,1792]{1,0:T(8,128)(2,1)S(1)}, bf16[128,1792]{1,0:T(8,128)(2,1)S(1)}, u32[]{:S(2)}, u32[]{:S(2)}) collective-permute-start(bf16[128,1792]{1,0:T(8,128)(2,1)S(1)} %combine.7), channel_id=1, source_target_pairs={{0,8},{2,10},{4,12},{6,14},{8,0},{10,2},{12,4},{14,6},{16,24},{18,... | collective-permute-start | bytes 1376264 | tf_op jit(solution)/shard_map/ppermute | solution.py:325
  140.4 9.2 %collective-permute-start.5 = (bf16[72,1792]{1,0:T(8,128)(2,1)S(1)}, bf16[72,1792]{1,0:T(8,128)(2,1)S(1)}, u32[]{:S(2)}, u32[]{:S(2)}) collective-permute-start(bf16[72,1792]{1,0:T(8,128)(2,1)S(1)} %get-tuple-element.47), channel_id=1, source_target_pairs={{0,2},{2,0},{4,6},{6,4},{8,10},{10,8},{12,14},{14,12},{16,18},{18,... | collective-permute-start | bytes 774152 | tf_op jit(solution)/shard_map/ppermute | solution.py:330
  141.2 11.4 %collective-permute-start.6 = (bf16[72,1792]{1,0:T(8,128)(2,1)S(1)}, bf16[72,1792]{1,0:T(8,128)(2,1)S(1)}, u32[]{:S(2)}, u32[]{:S(2)}) collective-permute-start(bf16[72,1792]{1,0:T(8,128)(2,1)S(1)} %get-tuple-element.48), channel_id=1, source_target_pairs={{0,4},{2,6},{4,0},{6,2},{8,12},{10,14},{12,8},{14,10},{16,20},{18,... | collective-permute-start | bytes 774152 | tf_op jit(solution)/shard_map/ppermute | solution.py:330
  142.6 11.8 %collective-permute-start.7 = (bf16[72,1792]{1,0:T(8,128)(2,1)S(1)}, bf16[72,1792]{1,0:T(8,128)(2,1)S(1)}, u32[]{:S(2)}, u32[]{:S(2)}) collective-permute-start(bf16[72,1792]{1,0:T(8,128)(2,1)S(1)} %get-tuple-element.49), channel_id=1, source_target_pairs={{0,6},{2,4},{4,2},{6,0},{8,14},{10,12},{12,10},{14,8},{16,22},{18,... | collective-permute-start | bytes 774152 | tf_op jit(solution)/shard_map/ppermute | solution.py:330
